TPU v7x, 32 devices: a whole 2x2x4 slice. The times are simulated.
32 devices in a mesh: row: 4 (over z), col: 8 (over y, x, core).
Axes of the slice: x: 2, y: 2, z: 4, core: 2. Of those that a mesh axis runs over, the one named last changes fastest.
Arguments:
- load_amp: float32 [2048, 4096], P('row', 'col'), may hold values from 0.05 to 1
- load_mask: int32 [2048, 4096], P('row', 'col'), may hold values 0 or 1
- leak: float32 [2048, 4096], P('row', 'col'), may hold values from 0.001 to 0.05
- coarse_leak: float32 [512, 1024], P('row', 'col'), may hold values from 0.01 to 0.5
- coarse_init: float32 [512, 1024], P('row', 'col'), may hold values from 0 to 1
- via_fine: int32 [4, 8192], P('row', 'col'), may hold values from 0 to 262143
- via_coarse: int32 [4, 8192], P('row', 'col'), may hold values from 0 to 131071, as said below
- via_count: int32 [4, 64], P('row', 'col'), may hold values from 0 to 128, as said below
Outputs:
- fine_drop: float32 [2048, 4096], P('row', 'col')
- coarse_drop: float32 [512, 1024], P('row', 'col')
Inputs may be any that keep to these rules, and one draw needn't show every extreme that they name: `via_coarse`: slot s of a tile names a coarse node whose stored column lies in s // 128 * 128 to s // 128 * 128 + 127. `via_count`: slots of an owner past its count are padding and carry arbitrary indices. In each tile row some owner gets 128 live slots from every tile of that row.
All inputs are finite; a program needn't handle non-finite values. No bound on the sum of `load_mask` on one device may be relied on, other than what follows from the above.
Results may differ from a plain program's by a relative error of at most 0.00022.
Values sent between devices are 32-bit elements; how exact they have to be, the bound alone decides.
A program may use at most 64 MiB of HBM per device.

v0:
```python
import functools
import jax
import jax.numpy as jnp
from jax import lax
from jax.experimental import pallas as pl
from jax.experimental.pallas import tpu as pltpu
from jax.sharding import PartitionSpec as P

GROUP = 16
ITERS = 4
LANES = 128
PAD = 16
EDGE = 8
HALF = LANES // 2
QUARTER = LANES // 4

via_conductance = 2.0
coarse_conductance = 4.0
relaxation = 0.8

F32 = jnp.float32
BF16 = jnp.bfloat16
MESH = pl.DeviceIdType.MESH


def divide(value, by):
    if by & (by - 1) == 0:
        return lax.shift_right_logical(value, by.bit_length() - 1)
    return value // by


def remainder(value, by):
    if by & (by - 1) == 0:
        return value & (by - 1)
    return value % by


def halves(value):
    high = value.astype(BF16).astype(F32)
    return high.astype(BF16), (value - high).astype(BF16)


def dot(a, b):
    return jnp.dot(a, b, preferred_element_type=F32)


def dot_t(a, b):
    return lax.dot_general(a, b, (((1,), (1,)), ((), ())), preferred_element_type=F32)


def fold(value):
    total = value[0:8]
    for n in range(1, value.shape[0] // 8):
        total = total + value[n * 8 : (n + 1) * 8]
    return total


def iota(shape, dim):
    return lax.broadcasted_iota(jnp.int32, shape, dim)


def kernel(
    R, C,
    amp_in, mask_in, leak_in, cleak_in, cinit_in, vf_in, vc_in, cnt_in,
    x_out, c_out,
    amp, mask, leak, cleak, cinit, vf, vc, cnt, load_sem,
    msg_out, msg_row, msg_ud, val_out, val_in, seen_out, seen_row, seen_ud,
    spot_v, spot, picked, lane_hot,
    row_hot, Bt, dv, D, dvq, Dq, V, Q, R0, rhs, rhsq,
    E, ET, H, rtop, rbot, rcorner,
    red_out, red_in,
    hot_own, hot_left, hot_right, hot_up, hot_down,
    coarse, turn, seam_out, crow_top, crow_bot, cleft, cright,
    send_sem, recv_sem,
):
    row, col = lax.axis_index("row"), lax.axis_index("col")
    TR, TC = leak_in.shape
    NB = TC // LANES
    EXT = TR + 2 * PAD
    BR, BC = cleak.shape
    S = vf.shape[1]
    per = S // C
    groups = BC // GROUP

    def cut(b):
        return pl.ds(b * LANES, LANES)

    loads = []

    def load(source, target):
        copy = pltpu.make_async_copy(source, target, load_sem.at[len(loads)])
        copy.start()
        loads.append(copy)
        return copy

    small = [load(cnt_in, cnt), load(vc_in, vc), load(vf_in, vf)]
    cinit_load = load(cinit_in, cinit)
    leak_loads = [load(leak_in.at[:, cut(b)], leak.at[b]) for b in range(NB)]
    cleak_load = load(cleak_in, cleak)
    amp_loads = [load(amp_in.at[:, cut(b)], amp.at[b]) for b in range(NB)]
    amp_loads += [load(mask_in.at[:, cut(b)], mask.at[b]) for b in range(NB)]

    up, down = lax.rem(row + R - 1, R), lax.rem(row + 1, R)
    left, right = lax.rem(col + C - 1, C), lax.rem(col + 1, C)
    top_ok, bot_ok = row > 0, row < R - 1
    left_ok, right_ok = col > 0, col < C - 1
    always = None

    barrier = pltpu.get_barrier_semaphore()

    def greet(r, c):
        pl.semaphore_signal(barrier, inc=1, device_id=(r, c), device_id_type=MESH)

    for d in range(1, C):
        greet(row, lax.rem(col + d, C))
    near_rows = R <= 4
    if near_rows:

        @pl.when(top_ok)
        def _():
            for d in range(C):
                greet(up, lax.rem(col + d, C))

        @pl.when(bot_ok)
        def _():
            for d in range(C):
                greet(down, lax.rem(col + d, C))
    else:
        for e in range(1, R):
            for d in range(C):
                greet(lax.rem(row + e, R), lax.rem(col + d, C))

    def welcome():
        if near_rows:
            rows = jnp.where(top_ok, 1, 0) + jnp.where(bot_ok, 1, 0)
            pl.semaphore_wait(barrier, C - 1 + C * rows)
        else:
            pl.semaphore_wait(barrier, R * C - 1)

    count = [0]
    pending = []

    def under(ok, body):
        if ok is always:
            body()
        else:
            pl.when(ok)(body)

    class Batch:
        def __init__(self, ok, heard, specs):
            self.ok, self.heard = ok, heard
            self.copies = []
            for src, dst, device in specs:
                n = count[0]
                count[0] += 1
                self.copies.append(pltpu.make_async_remote_copy(
                    src_ref=src, dst_ref=dst, send_sem=send_sem.at[n], recv_sem=recv_sem.at[n],
                    device_id=device, device_id_type=MESH,
                ))
            pending.append(self)

            def start():
                for copy in self.copies:
                    copy.start()

            under(ok, start)

        def land(self, otherwise=None):
            def wait():
                for copy in self.copies:
                    copy.wait_recv()

            under(self.heard, wait)
            if self.heard is not always and otherwise is not None:
                pl.when(jnp.logical_not(self.heard))(otherwise)

        def leave(self):
            def wait():
                for copy in self.copies:
                    copy.wait_send()

            under(self.ok, wait)

    for n in range(2):
        H[n] = jnp.zeros((LANES, TR), F32)
    for copy in small:
        copy.wait()
    lane = iota((1, per), 1)
    weight = jnp.concatenate(
        [jnp.where(lane < cnt[0, o], via_conductance, 0.0).astype(F32) for o in range(C)], axis=1
    )
    node = vc[...].astype(F32)
    for o in [-1] + list(range(C)) + [C]:
        part = slice((o % C) * per, (o % C + 1) * per)
        msg_out[o + 1, 0:1, :] = node[:, part]
        msg_out[o + 1, 1:2, :] = weight[:, part]
    msg_row[col] = msg_out[pl.ds(col, 3)]
    fine = vf[...]
    fine_row = divide(fine, TC)
    fine_col = remainder(fine, TC)
    spot_v[...] = divide(fine_col, LANES) * EXT + PAD + fine_row
    spot_copy = pltpu.make_async_copy(spot_v, spot, load_sem.at[len(loads)])
    spot_copy.start()
    step = 64

    def build_rows(i, carry):
        at = pl.ds(pl.multiple_of(i * step, step), step)
        place = iota((step, S), 0) + i * step
        row_hot[at, :] = jnp.where(place == fine_row, 1.0, 0.0).astype(BF16)
        return carry

    lax.fori_loop(0, TR // step, build_rows, 0)

    welcome()

    messages = Batch(always, always, [
        (msg_out.at[pl.ds(lax.rem(col + d, C), 3)], msg_row.at[col], (row, lax.rem(col + d, C)))
        for d in range(1, C)
    ])

    def seams(volt, n):
        turn[n] = volt.T
        seam_out[n, 0] = turn[n, pl.ds(0, groups, stride=GROUP), :]
        seam_out[n, 1] = turn[n, pl.ds(GROUP - 1, groups, stride=GROUP), :]

    def coarse_send(ref, n):
        return [
            Batch(top_ok, bot_ok, [(ref.at[pl.ds(0, 8)], crow_bot.at[n], (up, col))]),
            Batch(bot_ok, top_ok, [(ref.at[pl.ds(BR - 8, 8)], crow_top.at[n], (down, col))]),
            Batch(always, always, [
                (seam_out.at[n, 0], cright.at[n], (row, left)),
                (seam_out.at[n, 1], cleft.at[n], (row, right)),
            ]),
        ]

    def coarse_land(batches, n):
        def no_below():
            crow_bot[n] = jnp.zeros((8, BC), F32)

        def no_above():
            crow_top[n] = jnp.zeros((8, BC), F32)

        batches[0].land(no_below)
        batches[1].land(no_above)
        batches[2].land()

    cinit_load.wait()
    seams(cinit[...], 0)
    coarse0 = coarse_send(cinit, 0)
    messages_up = Batch(top_ok, bot_ok, [
        (msg_out.at[lax.rem(col + d, C) + 1], msg_ud.at[1, col], (up, lax.rem(col + d, C)))
        for d in range(C)
    ])
    messages_down = Batch(bot_ok, top_ok, [
        (msg_out.at[lax.rem(col + d, C) + 1], msg_ud.at[0, col], (down, lax.rem(col + d, C)))
        for d in range(C)
    ])

    lanes = iota((per, LANES), 1).astype(F32)
    for o in range(C):
        part = slice(o * per, (o + 1) * per)
        turned = jnp.broadcast_to(fine_col[:, part].astype(F32), (LANES, per)).T
        near = turned
        total = jnp.zeros((per, LANES), F32)
        for b in range(NB):
            hot = jnp.where(turned == lanes + b * LANES, 1.0, 0.0)
            Bt[part, b * LANES : (b + 1) * LANES] = hot.astype(BF16)
            total = total + hot
        lane_hot[part, :] = total

    zero_pad = jnp.zeros((8, LANES), F32)
    for n in range(ITERS):
        for b in range(NB):
            V[n, b * EXT : b * EXT + 8, :] = zero_pad
            V[n, (b + 1) * EXT - 8 : (b + 1) * EXT, :] = zero_pad
        for b in range(NB if n == 0 else 0):
            V[n, b * EXT + 8 : b * EXT + 16, :] = zero_pad
            V[n, (b + 1) * EXT - 16 : (b + 1) * EXT - 8, :] = zero_pad
        Q[n, 0:8, :] = zero_pad
        Q[n, EXT - 8 : EXT, :] = zero_pad
    for n in range(1, ITERS):
        for b in range(NB):
            V[n, b * EXT + 8 : b * EXT + 16, :] = zero_pad
            V[n, (b + 1) * EXT - 16 : (b + 1) * EXT - 8, :] = zero_pad

    for copy in leak_loads:
        copy.wait()
    wide_step = 256 if TR % 256 == 0 else step
    weight_low = weight.astype(BF16)

    def diagonal(i, carry):
        at = pl.ds(pl.multiple_of(i * wide_step, wide_step), wide_step)
        sums = dot(row_hot[at, :] * weight_low, Bt[...])
        for b in range(NB):
            inner = pl.ds(pl.multiple_of(b * EXT + PAD + i * wide_step, 8), wide_step)
            own = pl.ds(pl.multiple_of(b * TR + i * wide_step, 8), wide_step)
            value = 4.0 + leak[b, at, :] + sums[:, b * LANES : (b + 1) * LANES]
            D[own, :] = value
            dv[inner, :] = 1.0 / value
        return carry

    lax.fori_loop(0, TR // wide_step, diagonal, 0)

    lane_row = iota((8, LANES), 1)

    def wide(rows):
        return iota((rows, LANES), 1)

    def keep(ok, value):
        return value * jnp.where(ok, 1.0, 0.0).astype(F32)

    last = (NB - 1) * EXT

    def halo_send(F, n):
        edge = jnp.where(wide(TR) < HALF, F[PAD : PAD + TR, :], F[last + PAD : last + PAD + TR, :])
        E[n] = edge
        ET[n] = edge.T
        ends = [(PAD, up), (PAD + TR - EDGE, down)]
        sides = Batch(always, always, [
            (ET.at[n, pl.ds(0, EDGE)], H.at[n, pl.ds(HALF, EDGE)], (row, left)),
            (ET.at[n, pl.ds(LANES - EDGE, EDGE)], H.at[n, pl.ds(LANES - EDGE, EDGE)], (row, right)),
        ])
        above = Batch(top_ok, bot_ok, [
            (E.at[n, pl.ds(0, EDGE)], rcorner.at[n, 3], (up, left)),
            (E.at[n, pl.ds(0, EDGE)], rcorner.at[n, 2], (up, right)),
        ] + [
            (F.at[pl.ds(b * EXT + PAD, EDGE)], rbot.at[n, b], (up, col)) for b in range(NB)
        ])
        below = Batch(bot_ok, top_ok, [
            (E.at[n, pl.ds(TR - EDGE, EDGE)], rcorner.at[n, 1], (down, left)),
            (E.at[n, pl.ds(TR - EDGE, EDGE)], rcorner.at[n, 0], (down, right)),
        ] + [
            (F.at[pl.ds(b * EXT + PAD + TR - EDGE, EDGE)], rtop.at[n, b], (down, col)) for b in range(NB)
        ])
        return sides, above, below

    def edges_of(first, final, beyond):
        rows = first.shape[0]
        place = wide(rows)
        own = jnp.where(place < QUARTER, first, pltpu.roll(final, HALF, 1))
        if beyond is None:
            return own
        return jnp.where(place < HALF, own, beyond)

    def outer(right_side, left_side):
        place = wide(right_side.shape[0])
        return jnp.where(place < HALF + QUARTER, keep(right_ok, right_side), keep(left_ok, left_side))

    def halo_land(F, X, n, batches):
        sides, above, below = batches
        sides.land()
        side = H[n].T
        X[PAD : PAD + TR, :] = edges_of(
            F[PAD : PAD + TR, :], F[last + PAD : last + PAD + TR, :], outer(side, side)
        )

        def no_below():
            for b in range(NB):
                F[b * EXT + PAD + TR : b * EXT + PAD + TR + EDGE, :] = zero_pad
            X[PAD + TR : PAD + TR + EDGE, :] = zero_pad

        def no_above():
            for b in range(NB):
                F[b * EXT + PAD - EDGE : b * EXT + PAD, :] = zero_pad
            X[PAD - EDGE : PAD, :] = zero_pad

        above.land(no_below)
        below.land(no_above)

        @pl.when(bot_ok)
        def _():
            for b in range(NB):
                F[b * EXT + PAD + TR : b * EXT + PAD + TR + EDGE, :] = rbot[n, b]
            beyond = outer(pltpu.roll(rcorner[n, 3], HALF, 1), rcorner[n, 2])
            X[PAD + TR : PAD + TR + EDGE, :] = edges_of(rbot[n, 0], rbot[n, NB - 1], beyond)

        @pl.when(top_ok)
        def _():
            for b in range(NB):
                F[b * EXT + PAD - EDGE : b * EXT + PAD, :] = rtop[n, b]
            beyond = outer(pltpu.roll(rcorner[n, 1], HALF, 1), rcorner[n, 0])
            X[PAD - EDGE : PAD, :] = edges_of(rtop[n, 0], rtop[n, NB - 1], beyond)

    messages.land()

    def joined(pick):
        return jnp.concatenate([pick(t) for t in range(C)], axis=1)

    def places(pick):
        code = joined(pick).astype(jnp.int32)
        return divide(code, BC * C), remainder(code, BC)

    place_r = iota((BR, S), 0)
    place_c = iota((BC, S), 0)

    def one_hot(hit):
        return jnp.where(hit, 1.0, 0.0).astype(BF16)

    in_row, in_col = places(lambda t: msg_row[t, 1, 0:1, :])
    in_weight = joined(lambda t: msg_row[t, 1, 1:2, :])
    row_hit = place_r == in_row
    col_hot = one_hot(place_c == in_col)
    hot_own[...] = col_hot
    hi, lo = halves(cinit[...])
    seen = dot(hi, col_hot) + dot(lo, col_hot)
    at_via = jnp.sum(jnp.where(row_hit, seen, 0.0), axis=0, keepdims=True)
    for t in range(C):
        val_out[t] = at_via[:, t * per : (t + 1) * per]
    val_in[col] = val_out[col]
    values = Batch(always, always, [
        (val_out.at[lax.rem(col + d, C)], val_in.at[col], (row, lax.rem(col + d, C)))
        for d in range(1, C)
    ])

    dinv_copies = halo_send(dv, 0)

    def spread(hit, amount):
        hi, lo = halves(amount)
        zero = jnp.zeros((), BF16)
        return jnp.concatenate([jnp.where(hit, hi, zero), jnp.where(hit, lo, zero)], axis=0)

    cleak_load.wait()
    only = jnp.where(row_hit, in_weight, 0.0).astype(BF16)
    coarse_diag = 4.0 * coarse_conductance + cleak[...] + dot_t(only, col_hot)
    scale = relaxation / coarse_diag
    place = iota((BR, BC), 1)
    place_v = iota((BR, BC), 0)
    within = remainder(place, GROUP)
    group = iota((groups, BR), 0)

    def beside(volt, n, above, below, far_left, far_right):
        above = jnp.where(place_v == 0, keep(top_ok, above), pltpu.roll(volt, 1, 0))
        below = jnp.where(place_v == BR - 1, keep(bot_ok, below), pltpu.roll(volt, BR - 1, 0))
        turn[n, pl.ds(0, groups, stride=GROUP), :] = jnp.where(
            left_ok, far_left, jnp.where(group == 0, 0.0, jnp.roll(far_left, 1, 0))
        )
        turn[n, pl.ds(GROUP - 1, groups, stride=GROUP), :] = jnp.where(
            right_ok, far_right, jnp.where(group == groups - 1, 0.0, jnp.roll(far_right, -1, 0))
        )
        edge = turn[n].T
        before = jnp.where(within == 0, edge, pltpu.roll(volt, 1, 1))
        after = jnp.where(within == GROUP - 1, edge, pltpu.roll(volt, BC - 1, 1))
        return above + below + before + after

    coarse_land(coarse0, 0)
    volt = cinit[...]
    sides = beside(volt, 0, crow_top[0, 7:8, :], crow_bot[0, 0:1, :], cleft[0], cright[0])
    coarse[0] = volt + scale * (coarse_conductance * sides - coarse_diag * volt)
    coarse[1] = scale
    coarse[2] = coarse_diag
    coarse_later = []
    for n in range(2):
        seams(coarse[n], n + 1)
        coarse_later.append(coarse_send(coarse.at[n], n + 1))

    def quiet(ref, shape):
        def body():
            for t in range(C):
                ref[t] = jnp.zeros(shape, F32)
        return body

    messages_down.land(quiet(msg_ud.at[0], (2, per)))
    messages_up.land(quiet(msg_ud.at[1], (2, per)))
    left_row, left_col = places(lambda t: msg_row[t, 0, 0:1, :])
    right_row, right_col = places(lambda t: msg_row[t, 2, 0:1, :])
    above_row, above_col = places(lambda t: msg_ud[0, t, 0:1, :])
    below_row, below_col = places(lambda t: msg_ud[1, t, 0:1, :])
    hot_left[...] = one_hot(place_r == left_row)
    hot_right[...] = one_hot(place_r == right_row)
    hot_up[...] = one_hot(place_c == above_col)
    hot_down[...] = one_hot(place_c == below_col)

    def edge_copy(F, X, size):
        X[...] = edges_of(F[0:TR, :], F[(NB - 1) * size : (NB - 1) * size + TR, :], None)

    edge_copy(D, Dq, TR)
    halo_land(dv, dvq, 0, dinv_copies)

    for copy in amp_loads:
        copy.wait()
    values.land()
    drops = weight * joined(lambda o: val_in[o])
    drop_hi, drop_lo = halves(drops)
    half_step = 128 if TR % 128 == 0 else step

    def inject(i, carry):
        at = pl.ds(pl.multiple_of(i * half_step, half_step), half_step)
        hot = row_hot[at, :]
        added = dot(hot * drop_hi, Bt[...]) + dot(hot * drop_lo, Bt[...])
        for b in range(NB):
            inner = pl.ds(pl.multiple_of(b * EXT + PAD + i * half_step, 8), half_step)
            own = pl.ds(pl.multiple_of(b * TR + i * half_step, 8), half_step)
            value = amp[b, at, :] * mask[b, at, :].astype(F32) + added[:, b * LANES : (b + 1) * LANES]
            rhs[own, :] = value
            V[0, inner, :] = value * dv[inner, :]
        return carry

    lax.fori_loop(0, TR // half_step, inject, 0)
    first_copies = halo_send(V.at[0], 1)
    edge_copy(rhs, rhsq, TR)

    def stencil(k, start, size):
        place = wide(size)
        mids = [V[k, pl.ds(b * EXT + start, size), :] for b in range(NB)]
        lefts = [pltpu.roll(m, 1, 1) for m in mids]
        rights = [pltpu.roll(m, LANES - 1, 1) for m in mids]
        out = []
        for b in range(NB):
            tall = V[k, pl.ds(b * EXT + start - 1, size), :] + V[k, pl.ds(b * EXT + start + 1, size), :]
            before = jnp.where(place == 0, lefts[b - 1], lefts[b])
            after = jnp.where(place == LANES - 1, rights[(b + 1) % NB], rights[b])
            out.append(tall + (before + after))
        return mids, out

    def inward(b, value):
        place = wide(value.shape[0])
        if b == 0:
            value = jnp.where(place >= EDGE, value, 0.0)
        if b == NB - 1:
            value = jnp.where(place < LANES - EDGE, value, 0.0)
        return value

    def advance(k, start, size, totals):
        mids, near = stencil(k, start, size)
        totals = None if totals is None else list(totals)
        for b in range(NB):
            at = pl.ds(b * EXT + start, size)
            own = pl.ds(b * TR + start - PAD, size)
            if k < ITERS - 1:
                fresh = dv[at, :] * near[b]
                if k:
                    fresh = (fresh + fresh) - V[k - 1, at, :]
                V[k + 1, at, :] = fresh
                if totals is None:
                    continue
                if k == 0:
                    right_side = rhs[own, :]
                    applied = inward(b, right_side - near[b])
                    R0[own, :] = applied
                    totals[0] = totals[0] + fold(right_side * mids[b])
                    totals[1] = totals[1] + fold(applied * mids[b])
                    totals[2] = totals[2] + fold(applied * fresh)
                else:
                    totals[0] = totals[0] + fold(R0[own, :] * fresh)
            elif totals is not None:
                applied = inward(b, D[own, :] * mids[b] - near[b])
                totals[ITERS - 2] = totals[ITERS - 2] + fold(applied * mids[b])
                for j in range(1, ITERS - 1):
                    totals[j - 1] = totals[j - 1] + fold(applied * V[j, at, :])
        return None if totals is None else tuple(totals)

    def blank(n):
        return tuple(jnp.zeros((8, LANES), F32) for _ in range(n))

    kept = [3] + [1] * (ITERS - 2) + [ITERS - 1]
    chunk = 16
    sums = []
    for k in range(ITERS):
        if k < ITERS - 1:
            advance(k, PAD, EDGE, None)
            advance(k, PAD + TR - EDGE, EDGE, None)

        def body(i, carry, k=k):
            return advance(k, PAD + EDGE + i * chunk, chunk, carry)

        sums.append(lax.fori_loop(0, (TR - 2 * EDGE) // chunk, body, blank(kept[k])))

    halo_land(V.at[0], Q.at[0], 1, first_copies)
    for k in range(ITERS):
        if k < ITERS - 1:
            advance(k, PAD - EDGE, EDGE, None)
            advance(k, PAD + TR, EDGE, None)
        sums[k] = advance(k, PAD, EDGE, sums[k])
        sums[k] = advance(k, PAD + TR - EDGE, EDGE, sums[k])

    def rim(value):
        place = wide(value.shape[0])
        ours = (place < EDGE) | ((place >= HALF - EDGE) & (place < HALF))
        return jnp.where(ours, value, 0.0)

    def advance_edge(k, start, size, totals):
        mid = Q[k, pl.ds(start, size), :]
        near = Q[k, pl.ds(start - 1, size), :] + Q[k, pl.ds(start + 1, size), :]
        near = near + (pltpu.roll(mid, 1, 1) + pltpu.roll(mid, LANES - 1, 1))
        at = pl.ds(start, size)
        own = pl.ds(start - PAD, size)
        totals = None if totals is None else list(totals)
        if k < ITERS - 1:
            fresh = dvq[at, :] * near
            if k:
                fresh = (fresh + fresh) - Q[k - 1, at, :]
            Q[k + 1, at, :] = fresh
            if totals is not None:
                if k == 0:
                    applied = rim(rhsq[own, :] - near)
                    rhsq[own, :] = applied
                    totals[1] = totals[1] + fold(applied * mid)
                    totals[2] = totals[2] + fold(applied * fresh)
                else:
                    totals[0] = totals[0] + fold(rhsq[own, :] * fresh)
        elif totals is not None:
            applied = rim(Dq[own, :] * mid - near)
            totals[ITERS - 2] = totals[ITERS - 2] + fold(applied * mid)
            for j in range(1, ITERS - 1):
                totals[j - 1] = totals[j - 1] + fold(applied * Q[j, at, :])
        return None if totals is None else tuple(totals)

    edge_chunk = 64
    for k in range(ITERS):
        if k < ITERS - 1:
            advance_edge(k, PAD - EDGE, EDGE, None)
            advance_edge(k, PAD + TR, EDGE, None)

        def body(i, carry, k=k):
            return advance_edge(k, PAD + i * edge_chunk, edge_chunk, carry)

        sums[k] = lax.fori_loop(0, TR // edge_chunk, body, sums[k])

    flat = [total for part in sums for total in part]
    tile = jnp.concatenate([jnp.sum(total, axis=0, keepdims=True) for total in flat], axis=0)
    sub = iota((8, LANES), 0)
    number = len(flat)
    tile = jnp.sum(tile, axis=1, keepdims=True)
    red_out[...] = jnp.sum(jnp.where(sub == lane_row, tile, 0.0), axis=0, keepdims=True)
    me = row * C + col
    red_in[me] = red_out[...]
    reductions = Batch(always, always, [
        (red_out, red_in.at[me], (lax.rem(row + e, R), lax.rem(col + d, C)))
        for e in reversed(range(R)) for d in reversed(range(C)) if e or d
    ])

    def patch(i, carry):
        for k in range(1, ITERS):
            at = pl.ds(PAD + i * edge_chunk, edge_chunk)
            far = pl.ds(last + PAD + i * edge_chunk, edge_chunk)
            edge = Q[k, at, :]
            place = wide(edge_chunk)
            V[k, at, :] = jnp.where(place < EDGE, edge, V[k, at, :])
            V[k, far, :] = jnp.where(place >= LANES - EDGE, pltpu.roll(edge, HALF, 1), V[k, far, :])
        return carry

    lax.fori_loop(0, TR // edge_chunk, patch, 0)
    spot_copy.wait()
    unroll = 8

    def pick(i, carry):
        for n in range(unroll):
            s = i * unroll + n
            where = spot[0, s]
            for k in range(ITERS):
                picked[k, pl.ds(s, 1), :] = V[k, pl.ds(where, 1), :]
        return carry

    lax.fori_loop(0, S // unroll, pick, 0)
    diag_hit = iota((per, LANES), 0) == iota((per, LANES), 1)

    for o in range(C):
        part = slice(o * per, (o + 1) * per)
        hot = lane_hot[part, :]
        for k in range(ITERS):
            value = jnp.sum(picked[k, part, :] * hot, axis=1, keepdims=True)
            seen_out[o + 1, k : k + 1, :] = jnp.sum(jnp.where(diag_hit, value, 0.0), axis=0, keepdims=True)
    seen_out[0] = seen_out[C]
    seen_out[C + 1] = seen_out[1]
    seen_row[col] = seen_out[pl.ds(col, 3)]
    seen_side = Batch(always, always, [
        (seen_out.at[pl.ds(lax.rem(col + d, C), 3)], seen_row.at[col], (row, lax.rem(col + d, C)))
        for d in range(1, C)
    ])
    seen_up = Batch(top_ok, bot_ok, [
        (seen_out.at[lax.rem(col + d, C) + 1], seen_ud.at[1, col], (up, lax.rem(col + d, C)))
        for d in range(C)
    ])
    seen_down = Batch(bot_ok, top_ok, [
        (seen_out.at[lax.rem(col + d, C) + 1], seen_ud.at[0, col], (down, lax.rem(col + d, C)))
        for d in range(C)
    ])

    reductions.land()
    parts = [red_in[n] for n in range(R * C)]
    while len(parts) > 1:
        parts = [sum(parts[n : n + 2][1:], parts[n]) for n in range(0, len(parts), 2)]
    total = jnp.broadcast_to(parts[0], (8, LANES))
    total = jnp.sum(jnp.where(sub == lane_row, total, 0.0), axis=1, keepdims=True)
    scalar = [total[n : n + 1, :] for n in range(number)]
    energy = [scalar[1], scalar[2]] + scalar[3 : 3 + ITERS - 2]
    high = scalar[3 + ITERS - 2 :]
    for j in range(1, ITERS):
        energy.append(2.0 * high[j - 1] - energy[ITERS - 1 - j])
    moment = [scalar[0], scalar[0] - energy[0]]
    for n in range(2, ITERS):
        moment.append(2.0 * (moment[n - 1] - energy[n - 1]) - moment[n - 2])
    matrix = [[None] * (ITERS + 1) for _ in range(ITERS)]
    for j in range(ITERS):
        for k in range(j + 1):
            matrix[j][k] = matrix[k][j] = 0.5 * (energy[j + k] + energy[j - k])
        matrix[j][ITERS] = moment[j]
    for i in range(ITERS):
        inverse = 1.0 / matrix[i][i]
        for k in range(i + 1, ITERS + 1):
            matrix[i][k] = matrix[i][k] * inverse
        for j in range(i + 1, ITERS):
            for k in range(i + 1, ITERS + 1):
                matrix[j][k] = matrix[j][k] - matrix[j][i] * matrix[i][k]
    coef = [None] * ITERS
    for i in reversed(range(ITERS)):
        coef[i] = matrix[i][ITERS]
        for k in range(i + 1, ITERS):
            coef[i] = coef[i] - matrix[i][k] * coef[k]
    coef = [jnp.broadcast_to(c, (1, LANES)) for c in coef]

    def finish(i, carry):
        at = pl.ds(pl.multiple_of(i * step, step), step)
        for b in range(NB):
            inner = pl.ds(pl.multiple_of(b * EXT + PAD + i * step, 8), step)
            value = coef[0] * V[0, inner, :]
            for k in range(1, ITERS):
                value = value + coef[k] * V[k, inner, :]
            x_out[at, b * LANES : (b + 1) * LANES] = value
        return carry

    lax.fori_loop(0, TR // step, finish, 0)

    for n in range(2):
        coarse_land(coarse_later[n], n + 1)
    seen_side.land()
    seen_down.land(quiet(seen_ud.at[0], (ITERS, per)))
    seen_up.land(quiet(seen_ud.at[1], (ITERS, per)))

    def amount(value, weights):
        def one(t):
            seen = value(t)
            total = coef[0] * seen[0:1, :]
            for k in range(1, ITERS):
                total = total + coef[k] * seen[k : k + 1, :]
            return total * weights(t)
        return joined(one)

    def gathered(hit, value, weights, hot):
        out = dot_t(spread(hit, amount(value, weights)), hot)
        return out[: out.shape[0] // 2] + out[out.shape[0] // 2 :]

    place_g = iota((groups, S), 0) * GROUP
    one_row = iota((8, S), 0) == 0
    own_row, own_col = places(lambda t: msg_row[t, 1, 0:1, :])
    sources = gathered(
        place_r == own_row, lambda t: seen_row[t, 1], lambda t: msg_row[t, 1, 1:2, :], hot_own[...]
    )
    from_left = gathered(
        place_g + (GROUP - 1) == left_col, lambda t: seen_row[t, 0], lambda t: msg_row[t, 0, 1:2, :],
        hot_left[...],
    )
    from_right = gathered(
        place_g == right_col, lambda t: seen_row[t, 2], lambda t: msg_row[t, 2, 1:2, :], hot_right[...]
    )
    from_above = gathered(
        one_row & (above_row == BR - 1), lambda t: seen_ud[0, t], lambda t: msg_ud[0, t, 1:2, :], hot_up[...]
    )
    from_below = gathered(
        one_row & (below_row == 0), lambda t: seen_ud[1, t], lambda t: msg_ud[1, t, 1:2, :], hot_down[...]
    )
    scale = coarse[1]
    volt = coarse[0] + scale * sources
    sides = beside(
        volt, 0,
        crow_top[1, 7:8, :] + crow_top[2, 7:8, :] * from_above[0:1, :],
        crow_bot[1, 0:1, :] + crow_bot[2, 0:1, :] * from_below[0:1, :],
        cleft[1] + cleft[2] * from_left,
        cright[1] + cright[2] * from_right,
    )
    c_out[...] = volt + scale * (sources + coarse_conductance * sides - coarse[2] * volt)
    for batch in pending:
        batch.leave()


def per_device(R, C, load_amp, load_mask, leak, coarse_leak, coarse_init, via_fine, via_coarse, via_count):
    TR, TC = leak.shape
    BR, BC = coarse_leak.shape
    S = via_fine.shape[1]
    per = S // C
    NB = TC // LANES
    EXT = TR + 2 * PAD
    groups = BC // GROUP
    copies = 3 * (C - 1) + 4 * C + 2 * (2 + 2 * (2 + NB)) + 12 + R * C - 1
    vmem = pl.BlockSpec(memory_space=pltpu.VMEM)
    return pl.pallas_call(
        functools.partial(kernel, R, C),
        out_shape=(pltpu.VMEM((TR, TC), F32), pltpu.VMEM((BR, BC), F32)),
        in_specs=[pl.BlockSpec(memory_space=pltpu.HBM)] * 8,
        out_specs=(vmem, vmem),
        scratch_shapes=[
            pltpu.VMEM((NB, TR, LANES), F32), pltpu.VMEM((NB, TR, LANES), jnp.int32),
            pltpu.VMEM((NB, TR, LANES), F32),
            pltpu.VMEM((BR, BC), F32), pltpu.VMEM((BR, BC), F32),
            pltpu.VMEM((1, S), jnp.int32), pltpu.VMEM((1, S), jnp.int32),
            pltpu.SMEM((1, C), jnp.int32), pltpu.SemaphoreType.DMA((3 * NB + 6,)),
            pltpu.VMEM((C + 2, 2, per), F32), pltpu.VMEM((C, 3, 2, per), F32), pltpu.VMEM((2, C, 2, per), F32),
            pltpu.VMEM((C, 1, per), F32), pltpu.VMEM((C, 1, per), F32),
            pltpu.VMEM((C + 2, ITERS, per), F32), pltpu.VMEM((C, 3, ITERS, per), F32),
            pltpu.VMEM((2, C, ITERS, per), F32),
            pltpu.VMEM((1, S), jnp.int32), pltpu.SMEM((1, S), jnp.int32),
            pltpu.VMEM((ITERS, S, LANES), F32), pltpu.VMEM((S, LANES), F32),
            pltpu.VMEM((TR, S), BF16),
            pltpu.VMEM((S, TC), BF16),
            pltpu.VMEM((NB * EXT, LANES), F32),
            pltpu.VMEM((NB * TR, LANES), F32),
            pltpu.VMEM((EXT, LANES), F32),
            pltpu.VMEM((TR, LANES), F32),
            pltpu.VMEM((ITERS, NB * EXT, LANES), F32),
            pltpu.VMEM((ITERS, EXT, LANES), F32),
            pltpu.VMEM((NB * TR, LANES), F32),
            pltpu.VMEM((NB * TR, LANES), F32),
            pltpu.VMEM((TR, LANES), F32),
            pltpu.VMEM((2, TR, LANES), F32),
            pltpu.VMEM((2, LANES, TR), F32),
            pltpu.VMEM((2, LANES, TR), F32),
            pltpu.VMEM((2, NB, EDGE, LANES), F32),
            pltpu.VMEM((2, NB, EDGE, LANES), F32),
            pltpu.VMEM((2, 4, EDGE, LANES), F32),
            pltpu.VMEM((1, LANES), F32), pltpu.VMEM((R * C, 1, LANES), F32),
            pltpu.VMEM((BC, S), BF16), pltpu.VMEM((BR, S), BF16), pltpu.VMEM((BR, S), BF16),
            pltpu.VMEM((BC, S), BF16), pltpu.VMEM((BC, S), BF16),
            pltpu.VMEM((3, BR, BC), F32),
            pltpu.VMEM((3, BC, BR), F32), pltpu.VMEM((3, 2, groups, BR), F32),
            pltpu.VMEM((3, 8, BC), F32), pltpu.VMEM((3, 8, BC), F32),
            pltpu.VMEM((3, groups, BR), F32), pltpu.VMEM((3, groups, BR), F32),
            pltpu.SemaphoreType.DMA((copies,)),
            pltpu.SemaphoreType.DMA((copies,)),
        ],
        compiler_params=pltpu.CompilerParams(
            collective_id=0, has_side_effects=True, vmem_limit_bytes=58000 * 1024
        ),
    )(load_amp, load_mask, leak, coarse_leak, coarse_init, via_fine, via_coarse, via_count)


def solution(mesh):
    spec = P("row", "col")
    return jax.shard_map(
        functools.partial(per_device, mesh.shape["row"], mesh.shape["col"]),
        mesh=mesh, in_specs=(spec,) * 8, out_specs=(spec, spec), check_vma=False,
    )
```

profile of v0, /device:TPU:0, one launch (start us, length us, event | category | flops | bytes accessed | tf_op | source)
XLA Modules:
  0.0 43.9 jit_solution(10079683221884060036)
XLA Ops:
  0.6 41.7 %shard_map.95 = (f32[512,512]{1,0:T(8,128)S(1)}, f32[128,128]{1,0:T(8,128)S(1)}) custom-call(f32[512,512]{1,0:T(8,128)} %amp_in.1, s32[512,512]{1,0:T(8,128)} %mask_in.1, f32[512,512]{1,0:T(8,128)} %leak_in.1, f32[128,128]{1,0:T(8,128)} %cleak_in.1, f32[128,128]{1,0:T(8,128)} %cinit_in.1, s32[1,1024]{1,0:T(1,128)} %vf_in.1, s32[1,1024]{1,0:T(1,128)} %vc_in.1, ...), custom_call_target="tpu_custom_call" | custom-call | tf_op jit(solution)/shard_map/pallas_call | solution.py:786
  42.3 1.0 %copy.12 = f32[512,512]{1,0:T(8,128)} copy(f32[512,512]{1,0:T(8,128)S(1)} %get-tuple-element.2) | data formatting | bytes 2097152
  43.3 0.6 %copy.13 = f32[128,128]{1,0:T(8,128)} copy(f32[128,128]{1,0:T(8,128)S(1)} %get-tuple-element.3) | data formatting | bytes 131072
where the time goes:
time: 44.1 us; the launch traced here: 43.9 us
  Pallas kernels  41.7 us (95%)
  local copies, waits for them, and re-layouts  1.6 us (4%)
  between operations  0.64 us (1%)
    pallas_call x1, Pallas kernels, per_device(): pl.pallas_call(functools.partial(kernel, R, C), out_shape=(pltpu.VMEM((TR...  41.7 us
    unnamed x2, local copies, waits for them, and re-layouts  1.6 us

commit v1 on v0

--- a/solution.py
+++ b/solution.py
@@ -65,7 +65,7 @@
     x_out, c_out,
     amp, mask, leak, cleak, cinit, vf, vc, cnt, load_sem,
     msg_out, msg_row, msg_ud, val_out, val_in, seen_out, seen_row, seen_ud,
-    spot_v, spot, picked, lane_hot,
+    spot_v, spot, woven, picked, lane_hot,
     row_hot, Bt, dv, D, dvq, Dq, V, Q, R0, rhs, rhsq,
     E, ET, H, rtop, rbot, rcorner,
     red_out, red_in,
@@ -181,8 +181,6 @@
 
             under(self.ok, wait)
 
-    for n in range(2):
-        H[n] = jnp.zeros((LANES, TR), F32)
     for copy in small:
         copy.wait()
     lane = iota((1, per), 1)
@@ -198,7 +196,7 @@
     fine = vf[...]
     fine_row = divide(fine, TC)
     fine_col = remainder(fine, TC)
-    spot_v[...] = divide(fine_col, LANES) * EXT + PAD + fine_row
+    spot_v[...] = (divide(fine_col, LANES) * TR + fine_row) * ITERS
     spot_copy = pltpu.make_async_copy(spot_v, spot, load_sem.at[len(loads)])
     spot_copy.start()
     step = 64
@@ -344,7 +342,8 @@
 
     def outer(right_side, left_side):
         place = wide(right_side.shape[0])
-        return jnp.where(place < HALF + QUARTER, keep(right_ok, right_side), keep(left_ok, left_side))
+        right_side = jnp.where((place < HALF + EDGE) & right_ok, right_side, 0.0)
+        return jnp.where((place >= LANES - EDGE) & left_ok, left_side, right_side)
 
     def halo_land(F, X, n, batches):
         sides, above, below = batches
@@ -380,6 +379,8 @@
                 F[b * EXT + PAD - EDGE : b * EXT + PAD, :] = rtop[n, b]
             beyond = outer(pltpu.roll(rcorner[n, 1], HALF, 1), rcorner[n, 0])
             X[PAD - EDGE : PAD, :] = edges_of(rtop[n, 0], rtop[n, NB - 1], beyond)
+
+    dinv_copies = halo_send(dv, 0)
 
     messages.land()
 
@@ -412,8 +413,6 @@
         for d in range(1, C)
     ])
 
-    dinv_copies = halo_send(dv, 0)
-
     def spread(hit, amount):
         hi, lo = halves(amount)
         zero = jnp.zeros((), BF16)
@@ -481,7 +480,7 @@
     values.land()
     drops = weight * joined(lambda o: val_in[o])
     drop_hi, drop_lo = halves(drops)
-    half_step = 128 if TR % 128 == 0 else step
+    half_step = 256 if TR % 256 == 0 else step
 
     def inject(i, carry):
         at = pl.ds(pl.multiple_of(i * half_step, half_step), half_step)
@@ -553,7 +552,8 @@
         return tuple(jnp.zeros((8, LANES), F32) for _ in range(n))
 
     kept = [3] + [1] * (ITERS - 2) + [ITERS - 1]
-    chunk = 16
+    inside = TR - 2 * EDGE
+    chunk = inside // 2 if inside % 16 == 0 else inside
     sums = []
     for k in range(ITERS):
         if k < ITERS - 1:
@@ -563,7 +563,7 @@
         def body(i, carry, k=k):
             return advance(k, PAD + EDGE + i * chunk, chunk, carry)
 
-        sums.append(lax.fori_loop(0, (TR - 2 * EDGE) // chunk, body, blank(kept[k])))
+        sums.append(lax.fori_loop(0, inside // chunk, body, blank(kept[k])))
 
     halo_land(V.at[0], Q.at[0], 1, first_copies)
     for k in range(ITERS):
@@ -605,16 +605,13 @@
                 totals[j - 1] = totals[j - 1] + fold(applied * Q[j, at, :])
         return None if totals is None else tuple(totals)
 
-    edge_chunk = 64
+    edge_chunk = 128 if TR % 128 == 0 else step
     for k in range(ITERS):
         if k < ITERS - 1:
             advance_edge(k, PAD - EDGE, EDGE, None)
             advance_edge(k, PAD + TR, EDGE, None)
 
-        def body(i, carry, k=k):
-            return advance_edge(k, PAD + i * edge_chunk, edge_chunk, carry)
-
-        sums[k] = lax.fori_loop(0, TR // edge_chunk, body, sums[k])
+        sums[k] = advance_edge(k, PAD, TR, sums[k])
 
     flat = [total for part in sums for total in part]
     tile = jnp.concatenate([jnp.sum(total, axis=0, keepdims=True) for total in flat], axis=0)
@@ -623,6 +620,7 @@
     tile = jnp.sum(tile, axis=1, keepdims=True)
     red_out[...] = jnp.sum(jnp.where(sub == lane_row, tile, 0.0), axis=0, keepdims=True)
     me = row * C + col
+    early = len(pending)
     red_in[me] = red_out[...]
     reductions = Batch(always, always, [
         (red_out, red_in.at[me], (lax.rem(row + e, R), lax.rem(col + d, C)))
@@ -630,13 +628,19 @@
     ])
 
     def patch(i, carry):
-        for k in range(1, ITERS):
-            at = pl.ds(PAD + i * edge_chunk, edge_chunk)
-            far = pl.ds(last + PAD + i * edge_chunk, edge_chunk)
-            edge = Q[k, at, :]
-            place = wide(edge_chunk)
-            V[k, at, :] = jnp.where(place < EDGE, edge, V[k, at, :])
-            V[k, far, :] = jnp.where(place >= LANES - EDGE, pltpu.roll(edge, HALF, 1), V[k, far, :])
+        at = pl.ds(PAD + i * edge_chunk, edge_chunk)
+        place = wide(edge_chunk)
+        for b in range(NB):
+            here = pl.ds(b * EXT + PAD + i * edge_chunk, edge_chunk)
+            for k in range(ITERS):
+                value = V[k, here, :]
+                if k and b == 0:
+                    value = jnp.where(place < EDGE, Q[k, at, :], value)
+                if k and b == NB - 1:
+                    value = jnp.where(place >= LANES - EDGE, pltpu.roll(Q[k, at, :], HALF, 1), value)
+                if k and b in (0, NB - 1):
+                    V[k, here, :] = value
+                woven[pl.ds((b * TR + i * edge_chunk) * ITERS + k, edge_chunk, stride=ITERS), :] = value
         return carry
 
     lax.fori_loop(0, TR // edge_chunk, patch, 0)
@@ -647,8 +651,7 @@
         for n in range(unroll):
             s = i * unroll + n
             where = spot[0, s]
-            for k in range(ITERS):
-                picked[k, pl.ds(s, 1), :] = V[k, pl.ds(where, 1), :]
+            picked[pl.ds(pl.multiple_of(s * ITERS, ITERS), ITERS), :] = woven[pl.ds(where, ITERS), :]
         return carry
 
     lax.fori_loop(0, S // unroll, pick, 0)
@@ -658,7 +661,8 @@
         part = slice(o * per, (o + 1) * per)
         hot = lane_hot[part, :]
         for k in range(ITERS):
-            value = jnp.sum(picked[k, part, :] * hot, axis=1, keepdims=True)
+            mine = picked[pl.ds(o * per * ITERS + k, per, stride=ITERS), :]
+            value = jnp.sum(mine * hot, axis=1, keepdims=True)
             seen_out[o + 1, k : k + 1, :] = jnp.sum(jnp.where(diag_hit, value, 0.0), axis=0, keepdims=True)
     seen_out[0] = seen_out[C]
     seen_out[C + 1] = seen_out[1]
@@ -676,6 +680,8 @@
         for d in range(C)
     ])
 
+    for batch in pending[:early]:
+        batch.leave()
     reductions.land()
     parts = [red_in[n] for n in range(R * C)]
     while len(parts) > 1:
@@ -769,7 +775,7 @@
         cright[1] + cright[2] * from_right,
     )
     c_out[...] = volt + scale * (sources + coarse_conductance * sides - coarse[2] * volt)
-    for batch in pending:
+    for batch in pending[early:]:
         batch.leave()
 
 
@@ -799,7 +805,8 @@
             pltpu.VMEM((C + 2, ITERS, per), F32), pltpu.VMEM((C, 3, ITERS, per), F32),
             pltpu.VMEM((2, C, ITERS, per), F32),
             pltpu.VMEM((1, S), jnp.int32), pltpu.SMEM((1, S), jnp.int32),
-            pltpu.VMEM((ITERS, S, LANES), F32), pltpu.VMEM((S, LANES), F32),
+            pltpu.VMEM((NB * TR * ITERS, LANES), F32),
+            pltpu.VMEM((ITERS * S, LANES), F32), pltpu.VMEM((S, LANES), F32),
             pltpu.VMEM((TR, S), BF16),
             pltpu.VMEM((S, TC), BF16),
             pltpu.VMEM((NB * EXT, LANES), F32),

time: 44.1 us -> 30.5 us (0.69)
  Pallas kernels: 41.7 us -> 28.1 us
    pallas_call x1, Pallas kernels: 41.7 us -> 28.1 us  [per_device(): pl.pallas_call(functools.partial(kernel, R, C), out_shape=(pltpu.VMEM((TR...]
where the time goes in v1:
time: 30.5 us; the launch traced here: 30.3 us
  Pallas kernels  28.1 us (92%)
  local copies, waits for them, and re-layouts  1.6 us (5%)
  between operations  0.64 us (2%)
    pallas_call x1, Pallas kernels, per_device(): pl.pallas_call(functools.partial(kernel, R, C), out_shape=(pltpu.VMEM((TR...  28.1 us
    unnamed x2, local copies, waits for them, and re-layouts  1.6 us

profile of v1, /device:TPU:0, one launch (start us, length us, event | category | flops | bytes accessed | tf_op | source)
XLA Modules:
  0.0 30.3 jit_solution(6707980423225963516)
XLA Ops:
  0.6 28.1 %shard_map.95 = (f32[512,512]{1,0:T(8,128)S(1)}, f32[128,128]{1,0:T(8,128)S(1)}) custom-call(f32[512,512]{1,0:T(8,128)} %amp_in.1, s32[512,512]{1,0:T(8,128)} %mask_in.1, f32[512,512]{1,0:T(8,128)} %leak_in.1, f32[128,128]{1,0:T(8,128)} %cleak_in.1, f32[128,128]{1,0:T(8,128)} %cinit_in.1, s32[1,1024]{1,0:T(1,128)} %vf_in.1, s32[1,1024]{1,0:T(1,128)} %vc_in.1, ...), custom_call_target="tpu_custom_call" | custom-call | tf_op jit(solution)/shard_map/pallas_call | solution.py:792
  28.7 1.0 %copy.12 = f32[512,512]{1,0:T(8,128)} copy(f32[512,512]{1,0:T(8,128)S(1)} %get-tuple-element.2) | data formatting | bytes 2097152
  29.7 0.6 %copy.13 = f32[128,128]{1,0:T(8,128)} copy(f32[128,128]{1,0:T(8,128)S(1)} %get-tuple-element.3) | data formatting | bytes 131072

commit v2 on v1

--- a/solution.py
+++ b/solution.py
@@ -93,12 +93,19 @@
         loads.append(copy)
         return copy
 
+    def load_blocks(source, target):
+        sem = load_sem.at[len(loads)]
+        for b in range(NB):
+            pltpu.make_async_copy(source.at[:, cut(b)], target.at[b], sem).start()
+        copy = pltpu.make_async_copy(target, target, sem)
+        loads.append(copy)
+        return copy
+
     small = [load(cnt_in, cnt), load(vc_in, vc), load(vf_in, vf)]
-    cinit_load = load(cinit_in, cinit)
-    leak_loads = [load(leak_in.at[:, cut(b)], leak.at[b]) for b in range(NB)]
+    cinit_load = load(cinit_in, cinit.at[0])
+    leak_load = load_blocks(leak_in, leak)
     cleak_load = load(cleak_in, cleak)
-    amp_loads = [load(amp_in.at[:, cut(b)], amp.at[b]) for b in range(NB)]
-    amp_loads += [load(mask_in.at[:, cut(b)], mask.at[b]) for b in range(NB)]
+    amp_loads = [load_blocks(amp_in, amp), load_blocks(mask_in, mask)]
 
     up, down = lax.rem(row + R - 1, R), lax.rem(row + 1, R)
     left, right = lax.rem(col + C - 1, C), lax.rem(col + 1, C)
@@ -118,13 +125,11 @@
 
         @pl.when(top_ok)
         def _():
-            for d in range(C):
-                greet(up, lax.rem(col + d, C))
+            greet(up, col)
 
         @pl.when(bot_ok)
         def _():
-            for d in range(C):
-                greet(down, lax.rem(col + d, C))
+            greet(down, col)
     else:
         for e in range(1, R):
             for d in range(C):
@@ -133,7 +138,7 @@
     def welcome():
         if near_rows:
             rows = jnp.where(top_ok, 1, 0) + jnp.where(bot_ok, 1, 0)
-            pl.semaphore_wait(barrier, C - 1 + C * rows)
+            pl.semaphore_wait(barrier, C - 1 + rows)
         else:
             pl.semaphore_wait(barrier, R * C - 1)
 
@@ -147,39 +152,33 @@
             pl.when(ok)(body)
 
     class Batch:
-        def __init__(self, ok, heard, specs):
+        def __init__(self, ok, heard, whole, specs):
             self.ok, self.heard = ok, heard
-            self.copies = []
-            for src, dst, device in specs:
-                n = count[0]
-                count[0] += 1
-                self.copies.append(pltpu.make_async_remote_copy(
+            n = count[0]
+            count[0] += 1
+
+            def make(src, dst, device):
+                return pltpu.make_async_remote_copy(
                     src_ref=src, dst_ref=dst, send_sem=send_sem.at[n], recv_sem=recv_sem.at[n],
                     device_id=device, device_id_type=MESH,
-                ))
+                )
+
+            self.all = make(whole, whole, specs[0][2])
             pending.append(self)
 
             def start():
-                for copy in self.copies:
-                    copy.start()
+                for spec in specs:
+                    make(*spec).start()
 
             under(ok, start)
 
         def land(self, otherwise=None):
-            def wait():
-                for copy in self.copies:
-                    copy.wait_recv()
-
-            under(self.heard, wait)
+            under(self.heard, self.all.wait_recv)
             if self.heard is not always and otherwise is not None:
                 pl.when(jnp.logical_not(self.heard))(otherwise)
 
         def leave(self):
-            def wait():
-                for copy in self.copies:
-                    copy.wait_send()
-
-            under(self.ok, wait)
+            under(self.ok, self.all.wait_send)
 
     for copy in small:
         copy.wait()
@@ -211,7 +210,7 @@
 
     welcome()
 
-    messages = Batch(always, always, [
+    messages = Batch(always, always, msg_row.at[pl.ds(0, C - 1)], [
         (msg_out.at[pl.ds(lax.rem(col + d, C), 3)], msg_row.at[col], (row, lax.rem(col + d, C)))
         for d in range(1, C)
     ])
@@ -221,39 +220,31 @@
         seam_out[n, 0] = turn[n, pl.ds(0, groups, stride=GROUP), :]
         seam_out[n, 1] = turn[n, pl.ds(GROUP - 1, groups, stride=GROUP), :]
 
-    def coarse_send(ref, n):
+    def coarse_send(rows, n, m):
+        at = pl.ds(n, m)
         return [
-            Batch(top_ok, bot_ok, [(ref.at[pl.ds(0, 8)], crow_bot.at[n], (up, col))]),
-            Batch(bot_ok, top_ok, [(ref.at[pl.ds(BR - 8, 8)], crow_top.at[n], (down, col))]),
-            Batch(always, always, [
-                (seam_out.at[n, 0], cright.at[n], (row, left)),
-                (seam_out.at[n, 1], cleft.at[n], (row, right)),
+            Batch(top_ok, bot_ok, crow_bot.at[at], [(rows.at[:, pl.ds(0, 8)], crow_bot.at[at], (up, col))]),
+            Batch(bot_ok, top_ok, crow_top.at[at], [(rows.at[:, pl.ds(BR - 8, 8)], crow_top.at[at], (down, col))]),
+            Batch(always, always, seam_out.at[at], [
+                (seam_out.at[at, 0], cright.at[at], (row, left)),
+                (seam_out.at[at, 1], cleft.at[at], (row, right)),
             ]),
         ]
 
-    def coarse_land(batches, n):
+    def coarse_land(batches, n, m):
         def no_below():
-            crow_bot[n] = jnp.zeros((8, BC), F32)
+            crow_bot[n : n + m] = jnp.zeros((m, 8, BC), F32)
 
         def no_above():
-            crow_top[n] = jnp.zeros((8, BC), F32)
+            crow_top[n : n + m] = jnp.zeros((m, 8, BC), F32)
 
         batches[0].land(no_below)
         batches[1].land(no_above)
         batches[2].land()
 
     cinit_load.wait()
-    seams(cinit[...], 0)
-    coarse0 = coarse_send(cinit, 0)
-    messages_up = Batch(top_ok, bot_ok, [
-        (msg_out.at[lax.rem(col + d, C) + 1], msg_ud.at[1, col], (up, lax.rem(col + d, C)))
-        for d in range(C)
-    ])
-    messages_down = Batch(bot_ok, top_ok, [
-        (msg_out.at[lax.rem(col + d, C) + 1], msg_ud.at[0, col], (down, lax.rem(col + d, C)))
-        for d in range(C)
-    ])
-
+    seams(cinit[0], 0)
+    coarse0 = coarse_send(cinit, 0, 1)
     lanes = iota((per, LANES), 1).astype(F32)
     for o in range(C):
         part = slice(o * per, (o + 1) * per)
@@ -281,8 +272,7 @@
             V[n, b * EXT + 8 : b * EXT + 16, :] = zero_pad
             V[n, (b + 1) * EXT - 16 : (b + 1) * EXT - 8, :] = zero_pad
 
-    for copy in leak_loads:
-        copy.wait()
+    leak_load.wait()
     wide_step = 256 if TR % 256 == 0 else step
     weight_low = weight.astype(BF16)
 
@@ -313,24 +303,28 @@
         edge = jnp.where(wide(TR) < HALF, F[PAD : PAD + TR, :], F[last + PAD : last + PAD + TR, :])
         E[n] = edge
         ET[n] = edge.T
-        ends = [(PAD, up), (PAD + TR - EDGE, down)]
-        sides = Batch(always, always, [
+        sides = Batch(always, always, ET.at[n, pl.ds(0, 2 * EDGE)], [
             (ET.at[n, pl.ds(0, EDGE)], H.at[n, pl.ds(HALF, EDGE)], (row, left)),
             (ET.at[n, pl.ds(LANES - EDGE, EDGE)], H.at[n, pl.ds(LANES - EDGE, EDGE)], (row, right)),
         ])
-        above = Batch(top_ok, bot_ok, [
-            (E.at[n, pl.ds(0, EDGE)], rcorner.at[n, 3], (up, left)),
-            (E.at[n, pl.ds(0, EDGE)], rcorner.at[n, 2], (up, right)),
-        ] + [
+        above = Batch(top_ok, bot_ok, rbot.at[n], [
             (F.at[pl.ds(b * EXT + PAD, EDGE)], rbot.at[n, b], (up, col)) for b in range(NB)
         ])
-        below = Batch(bot_ok, top_ok, [
-            (E.at[n, pl.ds(TR - EDGE, EDGE)], rcorner.at[n, 1], (down, left)),
-            (E.at[n, pl.ds(TR - EDGE, EDGE)], rcorner.at[n, 0], (down, right)),
-        ] + [
+        below = Batch(bot_ok, top_ok, rtop.at[n], [
             (F.at[pl.ds(b * EXT + PAD + TR - EDGE, EDGE)], rtop.at[n, b], (down, col)) for b in range(NB)
         ])
         return sides, above, below
+
+    def corner_send(n):
+        above = Batch(top_ok, bot_ok, rcorner.at[n, pl.ds(2, 2)], [
+            (E.at[n, pl.ds(0, EDGE)], rcorner.at[n, 3], (up, left)),
+            (E.at[n, pl.ds(0, EDGE)], rcorner.at[n, 2], (up, right)),
+        ])
+        below = Batch(bot_ok, top_ok, rcorner.at[n, pl.ds(0, 2)], [
+            (E.at[n, pl.ds(TR - EDGE, EDGE)], rcorner.at[n, 1], (down, left)),
+            (E.at[n, pl.ds(TR - EDGE, EDGE)], rcorner.at[n, 0], (down, right)),
+        ])
+        return above, below
 
     def edges_of(first, final, beyond):
         rows = first.shape[0]
@@ -356,12 +350,10 @@
         def no_below():
             for b in range(NB):
                 F[b * EXT + PAD + TR : b * EXT + PAD + TR + EDGE, :] = zero_pad
-            X[PAD + TR : PAD + TR + EDGE, :] = zero_pad
 
         def no_above():
             for b in range(NB):
                 F[b * EXT + PAD - EDGE : b * EXT + PAD, :] = zero_pad
-            X[PAD - EDGE : PAD, :] = zero_pad
 
         above.land(no_below)
         below.land(no_above)
@@ -370,13 +362,31 @@
         def _():
             for b in range(NB):
                 F[b * EXT + PAD + TR : b * EXT + PAD + TR + EDGE, :] = rbot[n, b]
-            beyond = outer(pltpu.roll(rcorner[n, 3], HALF, 1), rcorner[n, 2])
-            X[PAD + TR : PAD + TR + EDGE, :] = edges_of(rbot[n, 0], rbot[n, NB - 1], beyond)
 
         @pl.when(top_ok)
         def _():
             for b in range(NB):
                 F[b * EXT + PAD - EDGE : b * EXT + PAD, :] = rtop[n, b]
+
+    def corner_land(X, n, batches):
+        above, below = batches
+
+        def no_below():
+            X[PAD + TR : PAD + TR + EDGE, :] = zero_pad
+
+        def no_above():
+            X[PAD - EDGE : PAD, :] = zero_pad
+
+        above.land(no_below)
+        below.land(no_above)
+
+        @pl.when(bot_ok)
+        def _():
+            beyond = outer(pltpu.roll(rcorner[n, 3], HALF, 1), rcorner[n, 2])
+            X[PAD + TR : PAD + TR + EDGE, :] = edges_of(rbot[n, 0], rbot[n, NB - 1], beyond)
+
+        @pl.when(top_ok)
+        def _():
             beyond = outer(pltpu.roll(rcorner[n, 1], HALF, 1), rcorner[n, 0])
             X[PAD - EDGE : PAD, :] = edges_of(rtop[n, 0], rtop[n, NB - 1], beyond)
 
@@ -402,13 +412,13 @@
     row_hit = place_r == in_row
     col_hot = one_hot(place_c == in_col)
     hot_own[...] = col_hot
-    hi, lo = halves(cinit[...])
+    hi, lo = halves(cinit[0])
     seen = dot(hi, col_hot) + dot(lo, col_hot)
     at_via = jnp.sum(jnp.where(row_hit, seen, 0.0), axis=0, keepdims=True)
     for t in range(C):
         val_out[t] = at_via[:, t * per : (t + 1) * per]
     val_in[col] = val_out[col]
-    values = Batch(always, always, [
+    values = Batch(always, always, val_in.at[pl.ds(0, C - 1)], [
         (val_out.at[lax.rem(col + d, C)], val_in.at[col], (row, lax.rem(col + d, C)))
         for d in range(1, C)
     ])
@@ -417,6 +427,17 @@
         hi, lo = halves(amount)
         zero = jnp.zeros((), BF16)
         return jnp.concatenate([jnp.where(hit, hi, zero), jnp.where(hit, lo, zero)], axis=0)
+
+    messages_up = Batch(top_ok, bot_ok, msg_ud.at[1], [
+        (msg_out.at[lax.rem(col + d, C) + 1], msg_ud.at[1, col], (up, lax.rem(col + d, C)))
+        for d in range(C)
+    ])
+    messages_down = Batch(bot_ok, top_ok, msg_ud.at[0], [
+        (msg_out.at[lax.rem(col + d, C) + 1], msg_ud.at[0, col], (down, lax.rem(col + d, C)))
+        for d in range(C)
+    ])
+
+    dinv_corners = corner_send(0)
 
     cleak_load.wait()
     only = jnp.where(row_hit, in_weight, 0.0).astype(BF16)
@@ -441,16 +462,15 @@
         after = jnp.where(within == GROUP - 1, edge, pltpu.roll(volt, BC - 1, 1))
         return above + below + before + after
 
-    coarse_land(coarse0, 0)
-    volt = cinit[...]
+    coarse_land(coarse0, 0, 1)
+    volt = cinit[0]
     sides = beside(volt, 0, crow_top[0, 7:8, :], crow_bot[0, 0:1, :], cleft[0], cright[0])
     coarse[0] = volt + scale * (coarse_conductance * sides - coarse_diag * volt)
     coarse[1] = scale
     coarse[2] = coarse_diag
-    coarse_later = []
     for n in range(2):
         seams(coarse[n], n + 1)
-        coarse_later.append(coarse_send(coarse.at[n], n + 1))
+    coarse_later = coarse_send(coarse.at[pl.ds(0, 2)], 1, 2)
 
     def quiet(ref, shape):
         def body():
@@ -458,16 +478,10 @@
                 ref[t] = jnp.zeros(shape, F32)
         return body
 
-    messages_down.land(quiet(msg_ud.at[0], (2, per)))
-    messages_up.land(quiet(msg_ud.at[1], (2, per)))
     left_row, left_col = places(lambda t: msg_row[t, 0, 0:1, :])
     right_row, right_col = places(lambda t: msg_row[t, 2, 0:1, :])
-    above_row, above_col = places(lambda t: msg_ud[0, t, 0:1, :])
-    below_row, below_col = places(lambda t: msg_ud[1, t, 0:1, :])
     hot_left[...] = one_hot(place_r == left_row)
     hot_right[...] = one_hot(place_r == right_row)
-    hot_up[...] = one_hot(place_c == above_col)
-    hot_down[...] = one_hot(place_c == below_col)
 
     def edge_copy(F, X, size):
         X[...] = edges_of(F[0:TR, :], F[(NB - 1) * size : (NB - 1) * size + TR, :], None)
@@ -480,7 +494,7 @@
     values.land()
     drops = weight * joined(lambda o: val_in[o])
     drop_hi, drop_lo = halves(drops)
-    half_step = 256 if TR % 256 == 0 else step
+    half_step = TR
 
     def inject(i, carry):
         at = pl.ds(pl.multiple_of(i * half_step, half_step), half_step)
@@ -491,11 +505,15 @@
             own = pl.ds(pl.multiple_of(b * TR + i * half_step, 8), half_step)
             value = amp[b, at, :] * mask[b, at, :].astype(F32) + added[:, b * LANES : (b + 1) * LANES]
             rhs[own, :] = value
-            V[0, inner, :] = value * dv[inner, :]
+            value = value * dv[inner, :]
+            V[0, inner, :] = value
+            woven[pl.ds((b * TR + i * half_step) * ITERS, half_step, stride=ITERS), :] = value
         return carry
 
     lax.fori_loop(0, TR // half_step, inject, 0)
     first_copies = halo_send(V.at[0], 1)
+    corner_land(dvq, 0, dinv_corners)
+    first_corners = corner_send(1)
     edge_copy(rhs, rhsq, TR)
 
     def stencil(k, start, size):
@@ -519,7 +537,8 @@
             value = jnp.where(place < LANES - EDGE, value, 0.0)
         return value
 
-    def advance(k, start, size, totals):
+    def advance(k, start, size, totals, start0=None):
+        start0 = start if start0 is None else start0
         mids, near = stencil(k, start, size)
         totals = None if totals is None else list(totals)
         for b in range(NB):
@@ -530,6 +549,8 @@
                 if k:
                     fresh = (fresh + fresh) - V[k - 1, at, :]
                 V[k + 1, at, :] = fresh
+                if PAD <= start0 < PAD + TR:
+                    woven[pl.ds((b * TR + start - PAD) * ITERS + k + 1, size, stride=ITERS), :] = fresh
                 if totals is None:
                     continue
                 if k == 0:
@@ -561,18 +582,12 @@
             advance(k, PAD + TR - EDGE, EDGE, None)
 
         def body(i, carry, k=k):
-            return advance(k, PAD + EDGE + i * chunk, chunk, carry)
+            return advance(k, PAD + EDGE + i * chunk, chunk, carry, PAD)
 
         sums.append(lax.fori_loop(0, inside // chunk, body, blank(kept[k])))
 
     halo_land(V.at[0], Q.at[0], 1, first_copies)
-    for k in range(ITERS):
-        if k < ITERS - 1:
-            advance(k, PAD - EDGE, EDGE, None)
-            advance(k, PAD + TR, EDGE, None)
-        sums[k] = advance(k, PAD, EDGE, sums[k])
-        sums[k] = advance(k, PAD + TR - EDGE, EDGE, sums[k])
-
+    corner_land(Q.at[0], 1, first_corners)
     def rim(value):
         place = wide(value.shape[0])
         ours = (place < EDGE) | ((place >= HALF - EDGE) & (place < HALF))
@@ -591,6 +606,14 @@
                 fresh = (fresh + fresh) - Q[k - 1, at, :]
             Q[k + 1, at, :] = fresh
             if totals is not None:
+                place = wide(size)
+                value = jnp.where(place < EDGE, fresh, V[k + 1, at, :])
+                V[k + 1, at, :] = value
+                woven[pl.ds((start - PAD) * ITERS + k + 1, size, stride=ITERS), :] = value
+                far = pl.ds(last + start, size)
+                value = jnp.where(place >= LANES - EDGE, pltpu.roll(fresh, HALF, 1), V[k + 1, far, :])
+                V[k + 1, far, :] = value
+                woven[pl.ds(((NB - 1) * TR + start - PAD) * ITERS + k + 1, size, stride=ITERS), :] = value
                 if k == 0:
                     applied = rim(rhsq[own, :] - near)
                     rhsq[own, :] = applied
@@ -605,12 +628,14 @@
                 totals[j - 1] = totals[j - 1] + fold(applied * Q[j, at, :])
         return None if totals is None else tuple(totals)
 
-    edge_chunk = 128 if TR % 128 == 0 else step
     for k in range(ITERS):
         if k < ITERS - 1:
+            advance(k, PAD - EDGE, EDGE, None)
+            advance(k, PAD + TR, EDGE, None)
             advance_edge(k, PAD - EDGE, EDGE, None)
             advance_edge(k, PAD + TR, EDGE, None)
-
+        sums[k] = advance(k, PAD, EDGE, sums[k])
+        sums[k] = advance(k, PAD + TR - EDGE, EDGE, sums[k])
         sums[k] = advance_edge(k, PAD, TR, sums[k])
 
     flat = [total for part in sums for total in part]
@@ -622,30 +647,13 @@
     me = row * C + col
     early = len(pending)
     red_in[me] = red_out[...]
-    reductions = Batch(always, always, [
+    reductions = Batch(always, always, red_in.at[pl.ds(0, R * C - 1)], [
         (red_out, red_in.at[me], (lax.rem(row + e, R), lax.rem(col + d, C)))
         for e in reversed(range(R)) for d in reversed(range(C)) if e or d
     ])
 
-    def patch(i, carry):
-        at = pl.ds(PAD + i * edge_chunk, edge_chunk)
-        place = wide(edge_chunk)
-        for b in range(NB):
-            here = pl.ds(b * EXT + PAD + i * edge_chunk, edge_chunk)
-            for k in range(ITERS):
-                value = V[k, here, :]
-                if k and b == 0:
-                    value = jnp.where(place < EDGE, Q[k, at, :], value)
-                if k and b == NB - 1:
-                    value = jnp.where(place >= LANES - EDGE, pltpu.roll(Q[k, at, :], HALF, 1), value)
-                if k and b in (0, NB - 1):
-                    V[k, here, :] = value
-                woven[pl.ds((b * TR + i * edge_chunk) * ITERS + k, edge_chunk, stride=ITERS), :] = value
-        return carry
-
-    lax.fori_loop(0, TR // edge_chunk, patch, 0)
     spot_copy.wait()
-    unroll = 8
+    unroll = 32
 
     def pick(i, carry):
         for n in range(unroll):
@@ -667,18 +675,26 @@
     seen_out[0] = seen_out[C]
     seen_out[C + 1] = seen_out[1]
     seen_row[col] = seen_out[pl.ds(col, 3)]
-    seen_side = Batch(always, always, [
+    seen_side = Batch(always, always, seen_row.at[pl.ds(0, C - 1)], [
         (seen_out.at[pl.ds(lax.rem(col + d, C), 3)], seen_row.at[col], (row, lax.rem(col + d, C)))
         for d in range(1, C)
     ])
-    seen_up = Batch(top_ok, bot_ok, [
+    seen_up = Batch(top_ok, bot_ok, seen_ud.at[1], [
         (seen_out.at[lax.rem(col + d, C) + 1], seen_ud.at[1, col], (up, lax.rem(col + d, C)))
         for d in range(C)
     ])
-    seen_down = Batch(bot_ok, top_ok, [
+    seen_down = Batch(bot_ok, top_ok, seen_ud.at[0], [
         (seen_out.at[lax.rem(col + d, C) + 1], seen_ud.at[0, col], (down, lax.rem(col + d, C)))
         for d in range(C)
     ])
+
+    messages_down.land(quiet(msg_ud.at[0], (2, per)))
+    messages_up.land(quiet(msg_ud.at[1], (2, per)))
+    above_row, above_col = places(lambda t: msg_ud[0, t, 0:1, :])
+    below_row, below_col = places(lambda t: msg_ud[1, t, 0:1, :])
+    hot_up[...] = one_hot(place_c == above_col)
+    hot_down[...] = one_hot(place_c == below_col)
+
 
     for batch in pending[:early]:
         batch.leave()
@@ -727,8 +743,7 @@
 
     lax.fori_loop(0, TR // step, finish, 0)
 
-    for n in range(2):
-        coarse_land(coarse_later[n], n + 1)
+    coarse_land(coarse_later, 1, 2)
     seen_side.land()
     seen_down.land(quiet(seen_ud.at[0], (ITERS, per)))
     seen_up.land(quiet(seen_ud.at[1], (ITERS, per)))
@@ -775,6 +790,7 @@
         cright[1] + cright[2] * from_right,
     )
     c_out[...] = volt + scale * (sources + coarse_conductance * sides - coarse[2] * volt)
+    assert count[0] == send_sem.shape[0]
     for batch in pending[early:]:
         batch.leave()
 
@@ -787,7 +803,7 @@
     NB = TC // LANES
     EXT = TR + 2 * PAD
     groups = BC // GROUP
-    copies = 3 * (C - 1) + 4 * C + 2 * (2 + 2 * (2 + NB)) + 12 + R * C - 1
+    batches = 24
     vmem = pl.BlockSpec(memory_space=pltpu.VMEM)
     return pl.pallas_call(
         functools.partial(kernel, R, C),
@@ -797,9 +813,9 @@
         scratch_shapes=[
             pltpu.VMEM((NB, TR, LANES), F32), pltpu.VMEM((NB, TR, LANES), jnp.int32),
             pltpu.VMEM((NB, TR, LANES), F32),
-            pltpu.VMEM((BR, BC), F32), pltpu.VMEM((BR, BC), F32),
+            pltpu.VMEM((BR, BC), F32), pltpu.VMEM((1, BR, BC), F32),
             pltpu.VMEM((1, S), jnp.int32), pltpu.VMEM((1, S), jnp.int32),
-            pltpu.SMEM((1, C), jnp.int32), pltpu.SemaphoreType.DMA((3 * NB + 6,)),
+            pltpu.SMEM((1, C), jnp.int32), pltpu.SemaphoreType.DMA((9,)),
             pltpu.VMEM((C + 2, 2, per), F32), pltpu.VMEM((C, 3, 2, per), F32), pltpu.VMEM((2, C, 2, per), F32),
             pltpu.VMEM((C, 1, per), F32), pltpu.VMEM((C, 1, per), F32),
             pltpu.VMEM((C + 2, ITERS, per), F32), pltpu.VMEM((C, 3, ITERS, per), F32),
@@ -831,8 +847,8 @@
             pltpu.VMEM((3, BC, BR), F32), pltpu.VMEM((3, 2, groups, BR), F32),
             pltpu.VMEM((3, 8, BC), F32), pltpu.VMEM((3, 8, BC), F32),
             pltpu.VMEM((3, groups, BR), F32), pltpu.VMEM((3, groups, BR), F32),
-            pltpu.SemaphoreType.DMA((copies,)),
-            pltpu.SemaphoreType.DMA((copies,)),
+            pltpu.SemaphoreType.DMA((batches,)),
+            pltpu.SemaphoreType.DMA((batches,)),
         ],
         compiler_params=pltpu.CompilerParams(
             collective_id=0, has_side_effects=True, vmem_limit_bytes=58000 * 1024

time: 30.5 us -> 27.9 us (0.915)
  Pallas kernels: 28.1 us -> 25.5 us
    pallas_call x1, Pallas kernels: 28.1 us -> 25.5 us  [per_device(): pl.pallas_call(functools.partial(kernel, R, C), out_shape=(pltpu.VMEM((TR...]
where the time goes in v2:
time: 27.9 us; the launch traced here: 27.7 us
  Pallas kernels  25.5 us (91%)
  local copies, waits for them, and re-layouts  1.6 us (6%)
  between operations  0.64 us (2%)
    pallas_call x1, Pallas kernels, per_device(): pl.pallas_call(functools.partial(kernel, R, C), out_shape=(pltpu.VMEM((TR...  25.5 us
    unnamed x2, local copies, waits for them, and re-layouts  1.6 us

profile of v2, /device:TPU:0, one launch (start us, length us, event | category | flops | bytes accessed | tf_op | source)
XLA Modules:
  0.0 27.7 jit_solution(6560285430319053333)
XLA Ops:
  0.6 25.5 %shard_map.95 = (f32[512,512]{1,0:T(8,128)S(1)}, f32[128,128]{1,0:T(8,128)S(1)}) custom-call(f32[512,512]{1,0:T(8,128)} %amp_in.1, s32[512,512]{1,0:T(8,128)} %mask_in.1, f32[512,512]{1,0:T(8,128)} %leak_in.1, f32[128,128]{1,0:T(8,128)} %cleak_in.1, f32[128,128]{1,0:T(8,128)} %cinit_in.1, s32[1,1024]{1,0:T(1,128)} %vf_in.1, s32[1,1024]{1,0:T(1,128)} %vc_in.1, ...), custom_call_target="tpu_custom_call" | custom-call | tf_op jit(solution)/shard_map/pallas_call | solution.py:808
  26.1 1.0 %copy.12 = f32[512,512]{1,0:T(8,128)} copy(f32[512,512]{1,0:T(8,128)S(1)} %get-tuple-element.2) | data formatting | bytes 2097152
  27.1 0.6 %copy.13 = f32[128,128]{1,0:T(8,128)} copy(f32[128,128]{1,0:T(8,128)S(1)} %get-tuple-element.3) | data formatting | bytes 131072

commit v3 on v2

--- a/solution.py
+++ b/solution.py
@@ -59,18 +59,45 @@
     return lax.broadcasted_iota(jnp.int32, shape, dim)
 
 
+def spread(hit, amount):
+    hi, lo = halves(amount)
+    zero = jnp.zeros((), BF16)
+    return jnp.concatenate([jnp.where(hit, hi, zero), jnp.where(hit, lo, zero)], axis=0)
+
+
+def beside(turn, R, C, volt, above, below, far_left, far_right):
+    row, col = lax.axis_index("row"), lax.axis_index("col")
+    BR, BC = volt.shape
+    groups = BC // GROUP
+    place_v = iota((BR, BC), 0)
+    within = remainder(iota((BR, BC), 1), GROUP)
+    group = iota((groups, BR), 0)
+    above = jnp.where(place_v == 0, jnp.where(row > 0, above, 0.0), pltpu.roll(volt, 1, 0))
+    below = jnp.where(place_v == BR - 1, jnp.where(row < R - 1, below, 0.0), pltpu.roll(volt, BR - 1, 0))
+    turn[pl.ds(0, groups, stride=GROUP), :] = jnp.where(
+        col > 0, far_left, jnp.where(group == 0, 0.0, jnp.roll(far_left, 1, 0))
+    )
+    turn[pl.ds(GROUP - 1, groups, stride=GROUP), :] = jnp.where(
+        col < C - 1, far_right, jnp.where(group == groups - 1, 0.0, jnp.roll(far_right, -1, 0))
+    )
+    edge = turn[...].T
+    before = jnp.where(within == 0, edge, pltpu.roll(volt, 1, 1))
+    after = jnp.where(within == GROUP - 1, edge, pltpu.roll(volt, BC - 1, 1))
+    return above + below + before + after
+
+
 def kernel(
     R, C,
     amp_in, mask_in, leak_in, cleak_in, cinit_in, vf_in, vc_in, cnt_in,
-    x_out, c_out,
+    x_out, coef_out, nodes, basis, coarse, beyond_rows, beyond_cols,
+    hot_own, hot_left, hot_right, hot_up, hot_down,
     amp, mask, leak, cleak, cinit, vf, vc, cnt, load_sem,
     msg_out, msg_row, msg_ud, val_out, val_in, seen_out, seen_row, seen_ud,
     spot_v, spot, woven, picked, lane_hot,
     row_hot, Bt, dv, D, dvq, Dq, V, Q, R0, rhs, rhsq,
     E, ET, H, rtop, rbot, rcorner,
     red_out, red_in,
-    hot_own, hot_left, hot_right, hot_up, hot_down,
-    coarse, turn, seam_out, crow_top, crow_bot, cleft, cright,
+    turn, seam_out, crow_top, crow_bot, cleft, cright,
     send_sem, recv_sem,
 ):
     row, col = lax.axis_index("row"), lax.axis_index("col")
@@ -423,11 +450,6 @@
         for d in range(1, C)
     ])
 
-    def spread(hit, amount):
-        hi, lo = halves(amount)
-        zero = jnp.zeros((), BF16)
-        return jnp.concatenate([jnp.where(hit, hi, zero), jnp.where(hit, lo, zero)], axis=0)
-
     messages_up = Batch(top_ok, bot_ok, msg_ud.at[1], [
         (msg_out.at[lax.rem(col + d, C) + 1], msg_ud.at[1, col], (up, lax.rem(col + d, C)))
         for d in range(C)
@@ -443,28 +465,9 @@
     only = jnp.where(row_hit, in_weight, 0.0).astype(BF16)
     coarse_diag = 4.0 * coarse_conductance + cleak[...] + dot_t(only, col_hot)
     scale = relaxation / coarse_diag
-    place = iota((BR, BC), 1)
-    place_v = iota((BR, BC), 0)
-    within = remainder(place, GROUP)
-    group = iota((groups, BR), 0)
-
-    def beside(volt, n, above, below, far_left, far_right):
-        above = jnp.where(place_v == 0, keep(top_ok, above), pltpu.roll(volt, 1, 0))
-        below = jnp.where(place_v == BR - 1, keep(bot_ok, below), pltpu.roll(volt, BR - 1, 0))
-        turn[n, pl.ds(0, groups, stride=GROUP), :] = jnp.where(
-            left_ok, far_left, jnp.where(group == 0, 0.0, jnp.roll(far_left, 1, 0))
-        )
-        turn[n, pl.ds(GROUP - 1, groups, stride=GROUP), :] = jnp.where(
-            right_ok, far_right, jnp.where(group == groups - 1, 0.0, jnp.roll(far_right, -1, 0))
-        )
-        edge = turn[n].T
-        before = jnp.where(within == 0, edge, pltpu.roll(volt, 1, 1))
-        after = jnp.where(within == GROUP - 1, edge, pltpu.roll(volt, BC - 1, 1))
-        return above + below + before + after
-
     coarse_land(coarse0, 0, 1)
     volt = cinit[0]
-    sides = beside(volt, 0, crow_top[0, 7:8, :], crow_bot[0, 0:1, :], cleft[0], cright[0])
+    sides = beside(turn.at[0], R, C, volt, crow_top[0, 7:8, :], crow_bot[0, 0:1, :], cleft[0], cright[0])
     coarse[0] = volt + scale * (coarse_conductance * sides - coarse_diag * volt)
     coarse[1] = scale
     coarse[2] = coarse_diag
@@ -575,6 +578,7 @@
     kept = [3] + [1] * (ITERS - 2) + [ITERS - 1]
     inside = TR - 2 * EDGE
     chunk = inside // 2 if inside % 16 == 0 else inside
+    piece = 8
     sums = []
     for k in range(ITERS):
         if k < ITERS - 1:
@@ -582,7 +586,9 @@
             advance(k, PAD + TR - EDGE, EDGE, None)
 
         def body(i, carry, k=k):
-            return advance(k, PAD + EDGE + i * chunk, chunk, carry, PAD)
+            for at in range(0, chunk, piece):
+                carry = advance(k, PAD + EDGE + i * chunk + at, min(piece, chunk - at), carry, PAD)
+            return carry
 
         sums.append(lax.fori_loop(0, inside // chunk, body, blank(kept[k])))
 
@@ -696,6 +702,28 @@
     hot_down[...] = one_hot(place_c == below_col)
 
 
+    coarse_land(coarse_later, 1, 2)
+    beyond_rows[0] = crow_top[1:3]
+    beyond_rows[1] = crow_bot[1:3]
+    beyond_cols[0] = cleft[1:3]
+    beyond_cols[1] = cright[1:3]
+    own_row, own_col = places(lambda t: msg_row[t, 1, 0:1, :])
+    for n, part in enumerate((own_row, left_col, right_col, above_row, below_row)):
+        nodes[n : n + 1, :] = part
+    seen_side.land()
+    seen_down.land(quiet(seen_ud.at[0], (ITERS, per)))
+    seen_up.land(quiet(seen_ud.at[1], (ITERS, per)))
+    heard = (
+        (lambda t: seen_row[t, 1], lambda t: msg_row[t, 1, 1:2, :]),
+        (lambda t: seen_row[t, 0], lambda t: msg_row[t, 0, 1:2, :]),
+        (lambda t: seen_row[t, 2], lambda t: msg_row[t, 2, 1:2, :]),
+        (lambda t: seen_ud[0, t], lambda t: msg_ud[0, t, 1:2, :]),
+        (lambda t: seen_ud[1, t], lambda t: msg_ud[1, t, 1:2, :]),
+    )
+    for n, (seen, weights) in enumerate(heard):
+        for t in range(C):
+            basis[n, :, t * per : (t + 1) * per] = seen(t) * weights(t)
+
     for batch in pending[:early]:
         batch.leave()
     reductions.land()
@@ -729,73 +757,65 @@
         coef[i] = matrix[i][ITERS]
         for k in range(i + 1, ITERS):
             coef[i] = coef[i] - matrix[i][k] * coef[k]
-    coef = [jnp.broadcast_to(c, (1, LANES)) for c in coef]
-
-    def finish(i, carry):
-        at = pl.ds(pl.multiple_of(i * step, step), step)
+    for k in range(ITERS):
+        coef[k] = jnp.broadcast_to(coef[k], (1, LANES))
+        coef_out[k : k + 1, :] = coef[k]
+    for at in range(0, TR, 8):
         for b in range(NB):
-            inner = pl.ds(pl.multiple_of(b * EXT + PAD + i * step, 8), step)
+            inner = pl.ds(b * EXT + PAD + at, 8)
             value = coef[0] * V[0, inner, :]
             for k in range(1, ITERS):
                 value = value + coef[k] * V[k, inner, :]
-            x_out[at, b * LANES : (b + 1) * LANES] = value
-        return carry
-
-    lax.fori_loop(0, TR // step, finish, 0)
-
-    coarse_land(coarse_later, 1, 2)
-    seen_side.land()
-    seen_down.land(quiet(seen_ud.at[0], (ITERS, per)))
-    seen_up.land(quiet(seen_ud.at[1], (ITERS, per)))
-
-    def amount(value, weights):
-        def one(t):
-            seen = value(t)
-            total = coef[0] * seen[0:1, :]
-            for k in range(1, ITERS):
-                total = total + coef[k] * seen[k : k + 1, :]
-            return total * weights(t)
-        return joined(one)
-
-    def gathered(hit, value, weights, hot):
-        out = dot_t(spread(hit, amount(value, weights)), hot)
+            x_out[at : at + 8, b * LANES : (b + 1) * LANES] = value
+    assert count[0] == send_sem.shape[0]
+    for batch in pending[early:]:
+        batch.leave()
+
+
+def finish(
+    R, C, x, coef, nodes, basis, coarse, beyond_rows, beyond_cols,
+    hot_own, hot_left, hot_right, hot_up, hot_down,
+    x_out, c_out, c, turn, sem,
+):
+    store = pltpu.make_async_copy(x, x_out, sem.at[0])
+    store.start()
+    BR, BC = c.shape
+    S = basis.shape[2]
+    groups = BC // GROUP
+    by = [jnp.concatenate([coef[k : k + 1, :]] * (S // LANES), axis=1) for k in range(ITERS)]
+
+    def gathered(n, hit, hot):
+        amount = by[0] * basis[n, 0:1, :]
+        for k in range(1, ITERS):
+            amount = amount + by[k] * basis[n, k : k + 1, :]
+        out = dot_t(spread(hit, amount), hot[...])
         return out[: out.shape[0] // 2] + out[out.shape[0] // 2 :]
 
     place_g = iota((groups, S), 0) * GROUP
     one_row = iota((8, S), 0) == 0
-    own_row, own_col = places(lambda t: msg_row[t, 1, 0:1, :])
-    sources = gathered(
-        place_r == own_row, lambda t: seen_row[t, 1], lambda t: msg_row[t, 1, 1:2, :], hot_own[...]
-    )
-    from_left = gathered(
-        place_g + (GROUP - 1) == left_col, lambda t: seen_row[t, 0], lambda t: msg_row[t, 0, 1:2, :],
-        hot_left[...],
-    )
-    from_right = gathered(
-        place_g == right_col, lambda t: seen_row[t, 2], lambda t: msg_row[t, 2, 1:2, :], hot_right[...]
-    )
-    from_above = gathered(
-        one_row & (above_row == BR - 1), lambda t: seen_ud[0, t], lambda t: msg_ud[0, t, 1:2, :], hot_up[...]
-    )
-    from_below = gathered(
-        one_row & (below_row == 0), lambda t: seen_ud[1, t], lambda t: msg_ud[1, t, 1:2, :], hot_down[...]
-    )
+    on_left = gathered(1, place_g + (GROUP - 1) == nodes[1:2, :], hot_left)
+    on_right = gathered(2, place_g == nodes[2:3, :], hot_right)
+    on_above = gathered(3, one_row & (nodes[3:4, :] == BR - 1), hot_up)
+    on_below = gathered(4, one_row & (nodes[4:5, :] == 0), hot_down)
+    sources = gathered(0, iota((BR, S), 0) == nodes[0:1, :], hot_own)
     scale = coarse[1]
     volt = coarse[0] + scale * sources
     sides = beside(
-        volt, 0,
-        crow_top[1, 7:8, :] + crow_top[2, 7:8, :] * from_above[0:1, :],
-        crow_bot[1, 0:1, :] + crow_bot[2, 0:1, :] * from_below[0:1, :],
-        cleft[1] + cleft[2] * from_left,
-        cright[1] + cright[2] * from_right,
+        turn, R, C, volt,
+        beyond_rows[0, 0, 7:8, :] + beyond_rows[0, 1, 7:8, :] * on_above[0:1, :],
+        beyond_rows[1, 0, 0:1, :] + beyond_rows[1, 1, 0:1, :] * on_below[0:1, :],
+        beyond_cols[0, 0] + beyond_cols[0, 1] * on_left,
+        beyond_cols[1, 0] + beyond_cols[1, 1] * on_right,
     )
-    c_out[...] = volt + scale * (sources + coarse_conductance * sides - coarse[2] * volt)
-    assert count[0] == send_sem.shape[0]
-    for batch in pending[early:]:
-        batch.leave()
+    c[...] = volt + scale * (sources + coarse_conductance * sides - coarse[2] * volt)
+    last = pltpu.make_async_copy(c, c_out, sem.at[1])
+    last.start()
+    store.wait()
+    last.wait()
 
 
 def per_device(R, C, load_amp, load_mask, leak, coarse_leak, coarse_init, via_fine, via_coarse, via_count):
+    inputs = (load_amp, load_mask, leak, coarse_leak, coarse_init, via_fine, via_coarse, via_count)
     TR, TC = leak.shape
     BR, BC = coarse_leak.shape
     S = via_fine.shape[1]
@@ -805,11 +825,17 @@
     groups = BC // GROUP
     batches = 24
     vmem = pl.BlockSpec(memory_space=pltpu.VMEM)
-    return pl.pallas_call(
+    state = pl.pallas_call(
         functools.partial(kernel, R, C),
-        out_shape=(pltpu.VMEM((TR, TC), F32), pltpu.VMEM((BR, BC), F32)),
+        out_shape=(
+            pltpu.VMEM((TR, TC), F32), pltpu.VMEM((8, LANES), F32), pltpu.VMEM((8, S), jnp.int32),
+            pltpu.VMEM((5, ITERS, S), F32), pltpu.VMEM((3, BR, BC), F32),
+            pltpu.VMEM((2, 2, 8, BC), F32), pltpu.VMEM((2, 2, groups, BR), F32),
+            pltpu.VMEM((BC, S), BF16), pltpu.VMEM((BR, S), BF16), pltpu.VMEM((BR, S), BF16),
+            pltpu.VMEM((BC, S), BF16), pltpu.VMEM((BC, S), BF16),
+        ),
         in_specs=[pl.BlockSpec(memory_space=pltpu.HBM)] * 8,
-        out_specs=(vmem, vmem),
+        out_specs=(vmem,) * 12,
         scratch_shapes=[
             pltpu.VMEM((NB, TR, LANES), F32), pltpu.VMEM((NB, TR, LANES), jnp.int32),
             pltpu.VMEM((NB, TR, LANES), F32),
@@ -841,9 +867,6 @@
             pltpu.VMEM((2, NB, EDGE, LANES), F32),
             pltpu.VMEM((2, 4, EDGE, LANES), F32),
             pltpu.VMEM((1, LANES), F32), pltpu.VMEM((R * C, 1, LANES), F32),
-            pltpu.VMEM((BC, S), BF16), pltpu.VMEM((BR, S), BF16), pltpu.VMEM((BR, S), BF16),
-            pltpu.VMEM((BC, S), BF16), pltpu.VMEM((BC, S), BF16),
-            pltpu.VMEM((3, BR, BC), F32),
             pltpu.VMEM((3, BC, BR), F32), pltpu.VMEM((3, 2, groups, BR), F32),
             pltpu.VMEM((3, 8, BC), F32), pltpu.VMEM((3, 8, BC), F32),
             pltpu.VMEM((3, groups, BR), F32), pltpu.VMEM((3, groups, BR), F32),
@@ -851,9 +874,19 @@
             pltpu.SemaphoreType.DMA((batches,)),
         ],
         compiler_params=pltpu.CompilerParams(
-            collective_id=0, has_side_effects=True, vmem_limit_bytes=58000 * 1024
+            collective_id=0, has_side_effects=True, vmem_limit_bytes=40000 * 1024
         ),
-    )(load_amp, load_mask, leak, coarse_leak, coarse_init, via_fine, via_coarse, via_count)
+    )(*(pltpu.with_memory_space_constraint(v, pltpu.HBM) for v in inputs))
+    return pl.pallas_call(
+        functools.partial(finish, R, C),
+        out_shape=(jax.ShapeDtypeStruct((TR, TC), F32), jax.ShapeDtypeStruct((BR, BC), F32)),
+        in_specs=[vmem] * 12,
+        out_specs=(pl.BlockSpec(memory_space=pltpu.HBM),) * 2,
+        scratch_shapes=[
+            pltpu.VMEM((BR, BC), F32), pltpu.VMEM((BC, BR), F32), pltpu.SemaphoreType.DMA((2,)),
+        ],
+        compiler_params=pltpu.CompilerParams(vmem_limit_bytes=16000 * 1024),
+    )(*(pltpu.with_memory_space_constraint(v, pltpu.VMEM) for v in state))
 
 
 def solution(mesh):

time: 27.9 us -> 25.7 us (0.921)
  local copies, waits for them, and re-layouts: 1.6 us -> 0 us
  Pallas kernels: 25.5 us -> 24.9 us
    pallas_call x1, Pallas kernels: 25.5 us -> 23.5 us  [per_device(): pl.pallas_call(functools.partial(kernel, R, C), out_shape=(pltpu.VMEM((TR...]
    unnamed x2 -> x0, local copies, waits for them, and re-layouts: 1.6 us -> none
    pallas_call x0 -> x1, Pallas kernels: none -> 1.38 us  [per_device(): pl.pallas_call(functools.partial(finish, R, C), out_shape=(jax.ShapeDtype...]
where the time goes in v3:
time: 25.7 us; the launch traced here: 25.6 us
  Pallas kernels  24.9 us (97%)
  between operations  0.64 us (2%)
    pallas_call x1, Pallas kernels, per_device(): pl.pallas_call(functools.partial(kernel, R, C), out_shape=(pltpu.VMEM((TR...  23.5 us
    pallas_call x1, Pallas kernels, per_device(): pl.pallas_call(functools.partial(finish, R, C), out_shape=(jax.ShapeDtype...  1.38 us

profile of v3, /device:TPU:0, one launch (start us, length us, event | category | flops | bytes accessed | tf_op | source)
XLA Modules:
  0.0 25.6 jit_solution(5025688388538127326)
XLA Ops:
  0.6 23.5 %shard_map.95 = (f32[512,512]{1,0:T(8,128)S(1)}, f32[8,128]{1,0:T(8,128)S(1)}, s32[8,1024]{1,0:T(8,128)S(1)}, f32[5,4,1024]{2,1,0:T(4,128)S(1)}, f32[3,128,128]{...) custom-call(f32[512,512]{1,0:T(8,128)} %amp_in.1, ...), custom_call_target="tpu_custom_call" | custom-call | tf_op jit(solution)/shard_map/pallas_call | solution.py:828
  24.2 1.4 %shard_map.96 = (f32[512,512]{1,0:T(8,128)}, f32[128,128]{1,0:T(8,128)}) custom-call(f32[512,512]{1,0:T(8,128)S(1)} %get-tuple-element.14.x, f32[8,128]{1,0:T(8,128)S(1)} %get-tuple-element.15.coef, s32[8,1024]{1,0:T(8,128)S(1)} %get-tuple-element.16.nodes, f32[5,4,1024]{2,1,0:T(4,128)S(1)} %get-tuple-element.17.basis, ...), custom_call_target="tpu_custom_call" | custom-call | tf_op jit(solution)/shard_map/pallas_call | solution.py:880

commit v4 on v3

--- a/solution.py
+++ b/solution.py
@@ -577,7 +577,7 @@
 
     kept = [3] + [1] * (ITERS - 2) + [ITERS - 1]
     inside = TR - 2 * EDGE
-    chunk = inside // 2 if inside % 16 == 0 else inside
+    chunk = inside
     piece = 8
     sums = []
     for k in range(ITERS):
@@ -612,14 +612,6 @@
                 fresh = (fresh + fresh) - Q[k - 1, at, :]
             Q[k + 1, at, :] = fresh
             if totals is not None:
-                place = wide(size)
-                value = jnp.where(place < EDGE, fresh, V[k + 1, at, :])
-                V[k + 1, at, :] = value
-                woven[pl.ds((start - PAD) * ITERS + k + 1, size, stride=ITERS), :] = value
-                far = pl.ds(last + start, size)
-                value = jnp.where(place >= LANES - EDGE, pltpu.roll(fresh, HALF, 1), V[k + 1, far, :])
-                V[k + 1, far, :] = value
-                woven[pl.ds(((NB - 1) * TR + start - PAD) * ITERS + k + 1, size, stride=ITERS), :] = value
                 if k == 0:
                     applied = rim(rhsq[own, :] - near)
                     rhsq[own, :] = applied
@@ -658,26 +650,36 @@
         for e in reversed(range(R)) for d in reversed(range(C)) if e or d
     ])
 
+    size = 64 if TR % 64 == 0 else EDGE
+    for k in range(1, ITERS):
+        for at in range(0, TR, size):
+            edge = Q[k, PAD + at : PAD + at + size, :]
+            place = wide(size)
+            for b, value in ((0, edge), (NB - 1, pltpu.roll(edge, HALF, 1))):
+                ours = place < EDGE if b == 0 else place >= LANES - EDGE
+                here = pl.ds(b * EXT + PAD + at, size)
+                value = jnp.where(ours, value, V[k, here, :])
+                V[k, here, :] = value
+                woven[pl.ds((b * TR + at) * ITERS + k, size, stride=ITERS), :] = value
     spot_copy.wait()
-    unroll = 32
-
-    def pick(i, carry):
-        for n in range(unroll):
-            s = i * unroll + n
-            where = spot[0, s]
-            picked[pl.ds(pl.multiple_of(s * ITERS, ITERS), ITERS), :] = woven[pl.ds(where, ITERS), :]
-        return carry
-
-    lax.fori_loop(0, S // unroll, pick, 0)
     diag_hit = iota((per, LANES), 0) == iota((per, LANES), 1)
 
-    for o in range(C):
-        part = slice(o * per, (o + 1) * per)
-        hot = lane_hot[part, :]
+    def pick(o):
+        for s in range(o * per, (o + 1) * per):
+            picked[s * ITERS : (s + 1) * ITERS, :] = woven[pl.ds(spot[0, s], ITERS), :]
+
+    def lanes_of(o):
+        hot = lane_hot[o * per : (o + 1) * per, :]
         for k in range(ITERS):
             mine = picked[pl.ds(o * per * ITERS + k, per, stride=ITERS), :]
             value = jnp.sum(mine * hot, axis=1, keepdims=True)
             seen_out[o + 1, k : k + 1, :] = jnp.sum(jnp.where(diag_hit, value, 0.0), axis=0, keepdims=True)
+
+    for o in range(C + 1):
+        if o < C:
+            pick(o)
+        if o:
+            lanes_of(o - 1)
     seen_out[0] = seen_out[C]
     seen_out[C + 1] = seen_out[1]
     seen_row[col] = seen_out[pl.ds(col, 3)]

time: 25.7 us -> 25 us (0.973)
  Pallas kernels: 24.9 us -> 24.2 us
    pallas_call x1, Pallas kernels: 23.5 us -> 22.9 us  [per_device(): pl.pallas_call(functools.partial(kernel, R, C), out_shape=(pltpu.VMEM((TR...]
where the time goes in v4:
time: 25 us; the launch traced here: 24.9 us
  Pallas kernels  24.2 us (97%)
  between operations  0.64 us (3%)
    pallas_call x1, Pallas kernels, per_device(): pl.pallas_call(functools.partial(kernel, R, C), out_shape=(pltpu.VMEM((TR...  22.9 us
    pallas_call x1, Pallas kernels, per_device(): pl.pallas_call(functools.partial(finish, R, C), out_shape=(jax.ShapeDtype...  1.38 us

profile of v4, /device:TPU:0, one launch (start us, length us, event | category | flops | bytes accessed | tf_op | source)
XLA Modules:
  0.0 24.9 jit_solution(10375692598880053703)
XLA Ops:
  0.6 22.9 %shard_map.95 = (f32[512,512]{1,0:T(8,128)S(1)}, f32[8,128]{1,0:T(8,128)S(1)}, s32[8,1024]{1,0:T(8,128)S(1)}, f32[5,4,1024]{2,1,0:T(4,128)S(1)}, f32[3,128,128]{...) custom-call(f32[512,512]{1,0:T(8,128)} %amp_in.1, ...), custom_call_target="tpu_custom_call" | custom-call | tf_op jit(solution)/shard_map/pallas_call | solution.py:830
  23.5 1.4 %shard_map.96 = (f32[512,512]{1,0:T(8,128)}, f32[128,128]{1,0:T(8,128)}) custom-call(f32[512,512]{1,0:T(8,128)S(1)} %get-tuple-element.14.x, f32[8,128]{1,0:T(8,128)S(1)} %get-tuple-element.15.coef, s32[8,1024]{1,0:T(8,128)S(1)} %get-tuple-element.16.nodes, f32[5,4,1024]{2,1,0:T(4,128)S(1)} %get-tuple-element.17.basis, ...), custom_call_target="tpu_custom_call" | custom-call | tf_op jit(solution)/shard_map/pallas_call | solution.py:882
